TPU v7x, 16 devices: a whole 2x2x2 slice. The times are simulated.
16 devices in a mesh: dp: 2 (over z), tp: 8 (over y, x, core).
Axes of the slice: x: 2, y: 2, z: 2, core: 2. Of those that a mesh axis runs over, the one named last changes fastest.
Arguments:
- x_in: bfloat16 [1024, 5120], P('dp'), parts along dimension 0
- lengths: int32 [1024], P('dp'), parts along dimension 0
- norm_gain: bfloat16 [2, 5120], replicated
- w_q: bfloat16 [2, 5120, 5120], P(None, None, 'tp')
- w_k: bfloat16 [2, 5120, 1024], P(None, None, 'tp')
- w_v: bfloat16 [2, 5120, 1024], P(None, None, 'tp')
- w_o: bfloat16 [2, 5120, 5120], P(None, 'tp')
- w_gate: bfloat16 [2, 5120, 13824], P(None, None, 'tp')
- w_up: bfloat16 [2, 5120, 13824], P(None, None, 'tp')
- w_down: bfloat16 [2, 13824, 5120], P(None, 'tp')
- k_cache: bfloat16 [2, 1024, 32, 8, 128], P(None, 'dp', None, 'tp'), parts along dimension 1
- v_cache: bfloat16 [2, 1024, 32, 8, 128], P(None, 'dp', None, 'tp'), parts along dimension 1
Outputs:
- output: bfloat16 [1024, 5120], P('dp'), parts along dimension 0
There are 2 independent parts. A program takes and returns all parts, laid end to end along the dimension named above; an argument that names none is the same for every part.
All inputs are finite; a program needn't handle non-finite values.
Results may differ from a plain program's by a relative error of at most 0.0174644.
Values are sent between devices in bfloat16 or wider.
A program may use at most 1 GiB of HBM per device.

v0:
```python
import jax
import jax.numpy as jnp
from jax import lax
from jax.sharding import PartitionSpec as P

NORM_EPS = 1e-5
ROPE_BASE = 500000.0


def rms_norm(x_res, gain_row):
    x_f32 = x_res.astype(jnp.float32)
    inv_rms = lax.rsqrt(jnp.mean(x_f32 * x_f32, axis=-1, keepdims=True) + NORM_EPS)
    return (x_f32 * inv_rms * gain_row.astype(jnp.float32)).astype(jnp.bfloat16)


def rope_rotate(head_vecs, positions):
    head_dim = head_vecs.shape[-1]
    half_dim = head_dim // 2
    inv_freq = 1.0 / (ROPE_BASE ** (jnp.arange(0, head_dim, 2).astype(jnp.float32) / head_dim))
    angles = positions.astype(jnp.float32)[:, None] * inv_freq[None, :]
    cos_ang = jnp.cos(angles)[:, None, :]
    sin_ang = jnp.sin(angles)[:, None, :]
    vec_f32 = head_vecs.astype(jnp.float32)
    rot_first = vec_f32[..., :half_dim]
    rot_second = vec_f32[..., half_dim:]
    return jnp.concatenate([rot_first * cos_ang - rot_second * sin_ang, rot_second * cos_ang + rot_first * sin_ang], axis=-1).astype(jnp.bfloat16)


def decode_attention(q_rot, k_rot, v_new, k_layer, v_layer, lengths):
    attn_scale = q_rot.shape[-1] ** -0.5
    seq_len = k_layer.shape[1]
    cache_logits = jnp.einsum('bkgd,bskd->bkgs', q_rot, k_layer, preferred_element_type=jnp.float32) * attn_scale
    valid_mask = jnp.arange(seq_len)[None, :] < lengths[:, None]
    cache_logits = jnp.where(valid_mask[:, None, None, :], cache_logits, -jnp.inf)
    self_logit = jnp.einsum('clhe,cle->clh', q_rot, k_rot, preferred_element_type=jnp.float32) * attn_scale
    row_peak = jnp.maximum(jnp.max(cache_logits, axis=-1), self_logit)
    cache_w = jnp.exp(cache_logits - row_peak[..., None])
    self_w = jnp.exp(self_logit - row_peak)
    prob_denom = jnp.sum(cache_w, axis=-1) + self_w
    cache_p = (cache_w / prob_denom[..., None]).astype(jnp.bfloat16)
    self_p = (self_w / prob_denom).astype(jnp.bfloat16)
    cache_part = jnp.einsum('bkgs,bskd->bkgd', cache_p, v_layer, preferred_element_type=jnp.float32)
    self_part = self_p.astype(jnp.float32)[..., None] * v_new.astype(jnp.float32)[:, :, None, :]
    return (cache_part + self_part).astype(jnp.bfloat16)


def layer_update(x_res, lengths, gain_row, wq_layer, wk_layer, wv_layer, wo_layer, wg_layer, wu_layer, wd_layer, k_layer, v_layer):
    tok_rows = x_res.shape[0]
    head_dim = k_layer.shape[-1]
    kv_local = k_layer.shape[-2]
    normed = rms_norm(x_res, gain_row)
    q_proj = jnp.dot(normed, wq_layer, preferred_element_type=jnp.float32).astype(jnp.bfloat16).reshape(tok_rows, -1, head_dim)
    k_proj = jnp.dot(normed, wk_layer, preferred_element_type=jnp.float32).astype(jnp.bfloat16).reshape(tok_rows, kv_local, head_dim)
    v_new = jnp.dot(normed, wv_layer, preferred_element_type=jnp.float32).astype(jnp.bfloat16).reshape(tok_rows, kv_local, head_dim)
    q_rot = rope_rotate(q_proj, lengths).reshape(tok_rows, kv_local, -1, head_dim)
    k_rot = rope_rotate(k_proj, lengths)
    attn_flat = decode_attention(q_rot, k_rot, v_new, k_layer, v_layer, lengths).reshape(tok_rows, -1)
    gate_act = jnp.dot(normed, wg_layer, preferred_element_type=jnp.float32).astype(jnp.bfloat16)
    up_act = jnp.dot(normed, wu_layer, preferred_element_type=jnp.float32).astype(jnp.bfloat16)
    mlp_hidden = (jax.nn.silu(gate_act.astype(jnp.float32)) * up_act.astype(jnp.float32)).astype(jnp.bfloat16)
    return jnp.dot(attn_flat, wo_layer, preferred_element_type=jnp.float32) + jnp.dot(mlp_hidden, wd_layer, preferred_element_type=jnp.float32)


def solution(mesh):
    tp_size = mesh.shape['tp']
    arg_specs = (P('dp', None), P('dp'), P(), P(None, None, 'tp'), P(None, None, 'tp'), P(None, None, 'tp'), P(None, 'tp', None), P(None, None, 'tp'), P(None, None, 'tp'), P(None, 'tp', None), P(None, 'dp', None, 'tp', None), P(None, 'dp', None, 'tp', None))

    def per_device(x_in, lengths, norm_gain, w_q, w_k, w_v, w_o, w_gate, w_up, w_down, k_cache, v_cache):
        tok_rows, model_width = x_in.shape
        col_width = model_width // tp_size
        col_start = lax.axis_index('tp') * col_width
        x_res = x_in
        for layer_idx in range(norm_gain.shape[0]):
            update = layer_update(x_res, lengths, norm_gain[layer_idx], w_q[layer_idx], w_k[layer_idx], w_v[layer_idx], w_o[layer_idx], w_gate[layer_idx], w_up[layer_idx], w_down[layer_idx], k_cache[layer_idx], v_cache[layer_idx])
            partial_sum = update.astype(jnp.bfloat16)
            received = lax.all_to_all(partial_sum, 'tp', 1, 0, tiled=True)
            reduced = jnp.sum(received.reshape(tp_size, tok_rows, col_width).astype(jnp.float32), axis=0)
            own_cols = lax.dynamic_slice_in_dim(x_res, col_start, col_width, axis=1)
            new_cols = (own_cols.astype(jnp.float32) + reduced).astype(jnp.bfloat16)
            x_res = lax.all_gather(new_cols, 'tp', axis=1, tiled=True)
        return x_res

    return jax.shard_map(per_device, mesh=mesh, in_specs=arg_specs, out_specs=P('dp', None), check_vma=False)
```

profile of v0, /device:TPU:0, one launch (start us, length us, event | category | flops | bytes accessed | tf_op | source)
XLA Modules:
  0.0 436.8 jit_solution(7985242807872340277)
XLA Ops:
  8.4 3.6 fusion.18
  17.3 5.3 %fusion.110 = f32[512,128]{1,0:T(8,128)} fusion(bf16[2,5120,128]{2,1,0:T(8,128)(2,1)} %param.17, bf16[512,5120]{1,0:T(8,128)(2,1)} %param.12, f32[5120]{0:T(1024)S(1)} %bitcast.188, f32[512]{0:T(512)S(1)} %add_rsqrt_fusion.1), kind=kOutput, calls=%fused_computation.112 | convolution fusion | flops 681705472 | bytes 6838272 | tf_op jit(solution)/shard_map/dot_general | solution.py:54
  22.6 7.1 %fusion.83 = f32[512,640]{1,0:T(8,128)S(1)} fusion(bf16[2,5120,640]{2,1,0:T(8,128)(2,1)} %param.15, bf16[512,5120]{1,0:T(8,128)(2,1)S(1)} %bitcast.173, f32[5120]{0:T(1024)S(1)} %bitcast.189, f32[512]{0:T(512)S(1)} %add_rsqrt_fusion.1), kind=kOutput, calls=%fused_computation.93 | convolution fusion | flops 3366584320 | bytes 13129728 | tf_op jit(solution)/shard_map/dot_general | solution.py:52
  32.2 15.8 %fusion.54 = bf16[512,1728]{0,1:T(8,128)(2,1)} fusion(bf16[2,5120,1728]{1,2,0:T(8,128)(2,1)} %param.19, bf16[512,5120]{1,0:T(8,128)(2,1)} %param.12, f32[5120]{0:T(1024)S(1)} %bitcast.190, f32[512]{0:T(512)S(1)} %add_rsqrt_fusion.1), kind=kOutput, calls=%fused_computation.68 | convolution fusion | flops 9071067136 | bytes 24729600 | tf_op jit(solution)/shard_map/dot_general | solution.py:58
  54.2 5.9 %fusion.74 = (f32[512,5]{1,0:T(8,128)S(1)}, f32[512,5,32]{2,1,0:T(8,128)}) fusion(pred[512,32]{1,0:T(8,128)(4,1)S(1)} %iota_compare_fusion, bf16[2,512,32,1,128]{4,2,1,3,0:T(8,128)(2,1)} %bitcast.170, bf16[512,5,64]{2,1,0:T(8,128)(2,1)S(1)} %get-tuple-element.8, bf16[512,5,64]{2,1,0:T(8,128)(2,1)S(1)} %get-tuple-element.7), kind=kOutput, calls=%fused_computation.86 | convolution fusion | flops 22525440 | bytes 5203968 | tf_op jit(solution)/shard_map/bkgd,bskd->bkgs/dot_general | solution.py:32
  65.4 6.0 %add_convert_fusion.4 = bf16[512,5,128]{2,1,0:T(8,128)(2,1)S(1)} fusion(bf16[2,512,32,1,128]{4,2,1,3,0:T(8,128)(2,1)} %bitcast.192, f32[512,5,32]{2,1,0:T(8,128)S(1)} %copy-done, f32[512,128]{1,0:T(8,128)} %fusion.110, f32[512,5]{1,0:T(8,128)} %copy.72, f32[512,5]{1,0:T(8,128)} %copy.70, f32[512,5]{1,0:T(8,128)S(1)} %copy.68, ...), kind=kOutput, calls=%fused_computation.80 | convolution fusion | flops 22364160 | bytes 5990400 | tf_op jit(solution)/shard_map/bkgs,bskd->bkgd/dot_general | solution.py:42
  72.0 17.0 %fusion.53.clone.5 = bf16[512,1728]{0,1:T(8,128)(2,1)} fusion(bf16[512,1728]{0,1:T(8,128)(2,1)} %fusion.54, bf16[2,5120,1728]{1,2,0:T(8,128)(2,1)} %param.20, bf16[512,5120]{1,0:T(8,128)(2,1)} %param.12, f32[5120]{0:T(1024)S(1)} %bitcast.191, f32[512]{0:T(512)S(1)} %add_rsqrt_fusion.1), kind=kOutput, calls=%fused_computation.67.clone.clone.clone.2 | convolution fusion | flops 9078145024 | bytes 26499072 | tf_op jit(solution)/shard_map/dot_general | solution.py:59
  89.0 9.7 %fusion.32 = f32[512,5120]{1,0:T(8,128)} fusion(bf16[512,640]{0,1:T(8,128)(2,1)S(1)} %bitcast.180, bf16[2,640,5120]{2,1,0:T(8,128)(2,1)} %param.18), kind=kOutput, calls=%fused_computation.36 | convolution fusion | flops 3355443200 | bytes 17694720 | tf_op jit(solution)/shard_map/dot_general | solution.py:61
  98.7 15.5 %add_convert_fusion.1 = bf16[512,5120]{1,0:T(8,128)(2,1)S(1)} fusion(f32[512,5120]{1,0:T(8,128)} %fusion.32, bf16[2,1728,5120]{2,1,0:T(8,128)(2,1)} %param.21, bf16[512,1728]{0,1:T(8,128)(2,1)} %fusion.53.clone.5), kind=kOutput, calls=%fused_computation.31 | convolution fusion | flops 9064939520 | bytes 35192832 | tf_op jit(solution)/shard_map/dot_general | solution.py:61
  117.0 5.5 %all-to-all-start = ((bf16[512,8,640]{2,0,1:T(8,128)(2,1)}), bf16[512,8,640]{2,0,1:T(8,128)(2,1)}, u32[]{:S(2)}, u32[]{:S(2)}) async-start(bf16[512,8,640]{2,0,1:T(8,128)(2,1)} %bitcast.168), calls=%async_computation | async-start | bytes 10485760 | tf_op jit(solution)/shard_map/all_to_all | solution.py:76
  122.5 60.4 %all-to-all-done = bf16[512,8,640]{2,0,1:T(8,128)(2,1)} async-done(((bf16[512,8,640]{2,0,1:T(8,128)(2,1)}), bf16[512,8,640]{2,0,1:T(8,128)(2,1)}, u32[]{:S(2)}, u32[]{:S(2)}) %all-to-all-start) | async-done | bytes 5242912 | tf_op jit(solution)/shard_map/all_to_all | solution.py:76
  188.7 36.8 %all-gather.3.cloned.1.call-done = bf16[512,5120]{1,0:T(8,128)(2,1)} async-done(((bf16[512,640]{1,0:T(8,128)(2,1)}), bf16[512,5120]{1,0:T(8,128)(2,1)}) %all-gather.3.cloned.1.call-update) | async-done | bytes 5242896 | tf_op jit(solution)/shard_map/all_gather | solution.py:80
  225.5 3.7 fusion.21
  233.0 8.2 %fusion.89 = f32[512,640]{1,0:T(8,128)S(1)} fusion(bf16[2,5120,640]{2,1,0:T(8,128)(2,1)} %param.15, bf16[512,5120]{1,0:T(8,128)(2,1)} %all-gather.3.cloned.1.call-done, f32[5120]{0:T(1024)S(1)} %bitcast.183, f32[512]{0:T(512)S(1)} %add_rsqrt_fusion), kind=kOutput, calls=%fused_computation.95 | convolution fusion | flops 3366584320 | bytes 13129728 | tf_op jit(solution)/shard_map/dot_general | solution.py:52
  246.7 4.7 %fusion.75 = (f32[512,5]{1,0:T(8,128)S(1)}, f32[512,5,32]{2,1,0:T(8,128)S(1)}) fusion(pred[512,32]{1,0:T(8,128)(4,1)S(1)} %iota_compare_fusion, bf16[2,512,32,1,128]{4,2,1,3,0:T(8,128)(2,1)} %bitcast.171, bf16[512,5,64]{2,1,0:T(8,128)(2,1)S(1)} %get-tuple-element.6, bf16[512,5,64]{2,1,0:T(8,128)(2,1)S(1)} %get-tuple-element.5), kind=kOutput, calls=%fused_computation.87 | convolution fusion | flops 22525440 | bytes 5203968 | tf_op jit(solution)/shard_map/bkgd,bskd->bkgs/dot_general | solution.py:32
  255.4 4.5 %fusion.119 = f32[512,128]{1,0:T(8,128)S(1)} fusion(bf16[2,5120,128]{2,1,0:T(8,128)(2,1)} %param.17, bf16[512,5120]{1,0:T(8,128)(2,1)} %all-gather.3.cloned.1.call-done, f32[5120]{0:T(1024)S(1)} %bitcast.184, f32[512]{0:T(512)S(1)} %add_rsqrt_fusion), kind=kOutput, calls=%fused_computation.115 | convolution fusion | flops 681705472 | bytes 6838272 | tf_op jit(solution)/shard_map/dot_general | solution.py:54
  259.8 4.2 add_convert_fusion.2
  265.7 10.1 %fusion.28 = f32[512,5120]{1,0:T(8,128)} fusion(bf16[512,640]{0,1:T(8,128)(2,1)S(1)} %bitcast.181, bf16[2,640,5120]{2,1,0:T(8,128)(2,1)} %param.18), kind=kOutput, calls=%fused_computation.32 | convolution fusion | flops 3355443200 | bytes 17694720 | tf_op jit(solution)/shard_map/dot_general | solution.py:61
  275.8 14.2 %fusion.60 = bf16[512,1728]{0,1:T(8,128)(2,1)} fusion(bf16[2,5120,1728]{1,2,0:T(8,128)(2,1)} %param.19, bf16[512,5120]{1,0:T(8,128)(2,1)S(1)} %bitcast.175, f32[5120]{0:T(1024)S(1)} %bitcast.185, f32[512]{0:T(512)S(1)} %add_rsqrt_fusion), kind=kOutput, calls=%fused_computation.70 | convolution fusion | flops 9071067136 | bytes 24729600 | tf_op jit(solution)/shard_map/dot_general | solution.py:58
  290.0 16.4 %fusion.52.clone.5 = bf16[512,1728]{0,1:T(8,128)(2,1)} fusion(bf16[512,1728]{0,1:T(8,128)(2,1)} %fusion.60, bf16[2,5120,1728]{1,2,0:T(8,128)(2,1)} %param.20, bf16[512,5120]{1,0:T(8,128)(2,1)} %all-gather.3.cloned.1.call-done, f32[5120]{0:T(1024)S(1)} %bitcast.186, f32[512]{0:T(512)S(1)} %add_rsqrt_fusion), kind=kOutput, calls=%fused_computation.66.clone.clone.clone.2 | convolution fusion | flops 9078145024 | bytes 26499072 | tf_op jit(solution)/shard_map/dot_general | solution.py:59
  306.4 15.7 %add_convert_fusion = bf16[512,5120]{1,0:T(8,128)(2,1)S(1)} fusion(f32[512,5120]{1,0:T(8,128)} %fusion.28, bf16[2,1728,5120]{2,1,0:T(8,128)(2,1)} %param.21, bf16[512,1728]{0,1:T(8,128)(2,1)} %fusion.52.clone.5), kind=kOutput, calls=%fused_computation.29 | convolution fusion | flops 9064939520 | bytes 35192832 | tf_op jit(solution)/shard_map/dot_general | solution.py:61
  322.6 62.8 %all_to_all.26 = bf16[512,8,640]{2,0,1:T(8,128)(2,1)S(1)} all-to-all(bf16[512,8,640]{2,0,1:T(8,128)(2,1)S(1)} %bitcast.169), channel_id=1, replica_groups=mesh['dp'=2,'tp'=8] {'tp'}, dimensions={1} | all-to-all | bytes 10485760 | tf_op jit(solution)/shard_map/all_to_all | solution.py:76
  388.2 36.2 %all-gather.5.cloned.1.call-done = bf16[512,5120]{1,0:T(8,128)(2,1)} async-done(((bf16[512,640]{1,0:T(8,128)(2,1)}), bf16[512,5120]{1,0:T(8,128)(2,1)}) %all-gather.5.cloned.1.call-update) | async-done | bytes 5242896 | tf_op jit(solution)/shard_map/all_gather | solution.py:80
  424.4 5.2 %copy.110 = bf16[512,5120]{1,0:T(8,128)(2,1)} copy(bf16[512,5120]{1,0:T(8,128)(2,1)} %all-gather.5.cloned.1.call-done) | data formatting | bytes 10485760
  (83 shorter events, 48.2 us)
Async XLA Ops:
  6.5 6.5 %copy-start.1 = (bf16[512,5120]{1,0:T(8,128)(2,1)S(1)}, bf16[512,5120]{1,0:T(8,128)(2,1)}, u32[]{:S(2)}) copy-start(bf16[512,5120]{1,0:T(8,128)(2,1)} %param.12) | copy-start | bytes 15728644
  6.5 5.4 %copy-start.6 = (bf16[2,5120]{1,0:T(2,128)(2,1)S(1)}, bf16[2,5120]{1,0:T(2,128)(2,1)}, u32[]{:S(2)}) copy-start(bf16[2,5120]{1,0:T(2,128)(2,1)} %param.14) | copy-start | bytes 61444
  13.0 37.0 %copy-start.3 = (f32[512,64]{1,0:T(8,128)}, f32[512,64]{1,0:T(8,128)S(1)}, u32[]{:S(2)}) copy-start(f32[512,64]{1,0:T(8,128)S(1)} %get-tuple-element.23) | copy-start | bytes 393220
  13.0 37.0 %copy-start.4 = (f32[512,64]{1,0:T(8,128)}, f32[512,64]{1,0:T(8,128)S(1)}, u32[]{:S(2)}) copy-start(f32[512,64]{1,0:T(8,128)S(1)} %get-tuple-element.24) | copy-start | bytes 393220
  17.1 5.5 %slice-start = ((s8[5242880]{0:T(1024)(128)(4,1)}), s8[1048576]{0:T(1024)(128)(4,1)S(1)}, s32[]{:S(2)}) async-start(s8[5242880]{0:T(1024)(128)(4,1)} %bitcast.172), calls=%async_computation.4 | async-start | bytes 2097152
  17.3 5.3 %slice-start.1 = ((s8[5242880]{0:T(1024)(128)(4,1)}), s8[4194304]{0:T(1024)(128)(4,1)S(1)}, s32[]{:S(2)}) async-start(s8[5242880]{0:T(1024)(128)(4,1)} %bitcast.172), calls=%async_computation.5 | async-start | bytes 8388608
  60.2 5.2 %copy-start = (f32[512,5,32]{2,1,0:T(8,128)S(1)}, f32[512,5,32]{2,1,0:T(8,128)}, u32[]{:S(2)}) copy-start(f32[512,5,32]{2,1,0:T(8,128)} %get-tuple-element.26) | copy-start | bytes 983044
  117.0 65.9 %all-to-all-start = ((bf16[512,8,640]{2,0,1:T(8,128)(2,1)}), bf16[512,8,640]{2,0,1:T(8,128)(2,1)}, u32[]{:S(2)}, u32[]{:S(2)}) async-start(bf16[512,8,640]{2,0,1:T(8,128)(2,1)} %bitcast.168), calls=%async_computation | async-start | bytes 10485760 | tf_op jit(solution)/shard_map/all_to_all | solution.py:76
  122.5 103.1 %all-gather.3.cloned.1.call-start = ((), (), s32[]{:S(2)}) async-start(), calls=%async_computation.2 | async-start | bytes 5898240 | tf_op jit(solution)/shard_map/all_gather | solution.py:80
  186.2 43.0 %copy-start.7 = (bf16[2,5120,128]{2,1,0:T(8,128)(2,1)S(1)}, bf16[2,5120,128]{2,1,0:T(8,128)(2,1)}, u32[]{:S(2)}) copy-start(bf16[2,5120,128]{2,1,0:T(8,128)(2,1)} %param.16) | copy-start | bytes 7864324
  188.5 235.9 %all-gather.5.cloned.1.call-start = ((), (), s32[]{:S(2)}) async-start(), calls=%async_computation.3 | async-start | bytes 5898240 | tf_op jit(solution)/shard_map/all_gather | solution.py:80
  225.5 4.0 copy-start.2
  246.7 4.8 %copy-start.5 = (f32[512,128]{1,0:T(8,128)S(1)}, f32[512,128]{1,0:T(8,128)}, u32[]{:S(2)}) copy-start(f32[512,128]{1,0:T(8,128)} %copy.102) | copy-start | bytes 786436
  264.0 11.7 %slice-start.2 = ((s8[5242880]{0:T(1024)(128)(4,1)}), s8[1048576]{0:T(1024)(128)(4,1)S(1)}, s32[]{:S(2)}) async-start(s8[5242880]{0:T(1024)(128)(4,1)} %bitcast.174), calls=%async_computation.6 | async-start | bytes 2097152
  265.7 10.1 %slice-start.3 = ((s8[5242880]{0:T(1024)(128)(4,1)}), s8[4194304]{0:T(1024)(128)(4,1)S(1)}, s32[]{:S(2)}) async-start(s8[5242880]{0:T(1024)(128)(4,1)} %bitcast.174), calls=%async_computation.7 | async-start | bytes 8388608
Sparse Core Ops, SparseCore 0:
  188.6 36.8 all-gather.2
  388.3 35.9 all-gather.4
where the time goes:
time: 444 us; the launch traced here: 437 us
  matrix products  166 us (37%)
  waiting for transfers between devices  133 us (30%)
  blocking collectives  62.8 us (14%)
  other arithmetic  32.2 us (7%)
  local copies, waits for them, and re-layouts  22.7 us (5%)
  between operations  14.2 us (3%)
  starting transfers between devices  5.71 us (1%)
    all_gather x2, waiting for transfers between devices, per_device(): x_res = lax.all_gather(new_cols, 'tp', axis=1, tiled=True)  72.9 us
    all_to_all x1, blocking collectives, per_device(): received = lax.all_to_all(partial_sum, 'tp', 1, 0, tiled=True)  62.8 us
    all_to_all x1, waiting for transfers between devices, per_device(): received = lax.all_to_all(partial_sum, 'tp', 1, 0, tiled=True)  60.4 us
    dot_general x2, matrix products, layer_update(): jnp.dot(normed, wu_layer, preferred_element_type=jnp.float32)  33.3 us
    dot_general x2, matrix products, layer_update(): jnp.dot(mlp_hidden, wd_layer, preferred_element_type=jnp.float32)  31.2 us
    dot_general x2, matrix products, layer_update(): jnp.dot(normed, wg_layer, preferred_element_type=jnp.float32)  30.1 us
    dot_general x2, matrix products, layer_update(): jnp.dot(attn_flat, wo_layer, preferred_element_type=jnp.float32)  19.8 us
    dot_general x2, matrix products, layer_update(): jnp.dot(normed, wq_layer, preferred_element_type=jnp.float32)  15.4 us
  transfers between devices with their start and end apart: 3, of which 3 were waited for; matrix products, arithmetic and copies ran while one was open for 0% of the time, Pallas kernels for 0%

commit v1 on v0

v1 whole, which is shorter than its diff:
```python
import functools

import jax
import jax.numpy as jnp
from jax import lax
from jax.experimental import pallas as pl
from jax.experimental.pallas import tpu as pltpu
from jax.sharding import PartitionSpec as P

NORM_EPS = 1e-5
ROPE_BASE = 500000.0
MESH = pl.DeviceIdType.MESH
BF, F32 = jnp.bfloat16, jnp.float32
NT_DIMS = (((1,), (1,)), ((), ()))


def attend_block(t0, qkv, cos, sin, bound, keys, vals, groups, head, seq):
    rows = pl.ds(t0, 8)
    cached = pl.ds(pl.multiple_of(t0 * seq, 8 * seq), 8 * seq)
    scale = head ** -0.5
    c, s = cos[rows, :], sin[rows, :]
    proj = qkv[rows, :].astype(BF).astype(F32)

    def turn(v):
        return (v * c + pltpu.roll(v, head // 2, 1) * s).astype(BF).astype(F32)

    q = jnp.concatenate([turn(proj[:, head * h:head * (h + 1)]) for h in range(groups)], axis=0)
    k_new = turn(proj[:, groups * head:(groups + 1) * head])
    v_new = proj[:, (groups + 1) * head:]
    logits = lax.dot_general(q.astype(BF), keys[cached, :], NT_DIMS, preferred_element_type=F32) * scale
    logits = logits.reshape(groups, 8, 8 * seq)
    own = jnp.sum(q.reshape(groups, 8, head) * k_new[None], axis=-1, keepdims=True) * scale
    col = lax.broadcasted_iota(jnp.int32, (8, 8 * seq), 1)
    low = lax.broadcasted_iota(jnp.int32, (8, 8 * seq), 0) * seq
    high = jnp.concatenate([bound[rows, :]] * (8 * seq // 128), axis=1) + low
    logits = jnp.where(((col >= low) & (col < high))[None], logits, -jnp.inf)
    peak = jnp.maximum(jnp.max(logits, axis=-1, keepdims=True), own)
    w = jnp.exp(logits - peak)
    w_own = jnp.exp(own - peak)
    inv = 1.0 / (jnp.sum(w, axis=-1, keepdims=True) + w_own)
    p = (w * inv).reshape(groups * 8, 8 * seq).astype(BF)
    p_own = (w_own * inv).astype(BF).astype(F32)
    out = jnp.dot(p, vals[cached, :], preferred_element_type=F32).reshape(groups, 8, head)
    return out + p_own * v_new[None]


def front_kernel(layer, dims, x_hbm, bound, cos, sin, gain, wq, wk, wv, wg, wu, kc, vc, h_ref,
                 x, a, inv_ref, qkv_w, gate_w, up_w, qkv, gate, up, keys, vals, x_sem, w_sem, kv_sem):
    groups, head, seq, kb, steps = dims
    qw = groups * head
    rows, ff = x.shape[0], gate.shape[1]

    def weights(step, slot):
        ks = pl.ds(pl.multiple_of(step * kb, kb), kb)
        pairs = (
            (wq.at[layer, ks, :], qkv_w.at[slot, :, 0:qw]),
            (wk.at[layer, ks, :], qkv_w.at[slot, :, qw:qw + head]),
            (wv.at[layer, ks, :], qkv_w.at[slot, :, qw + head:qw + 2 * head]),
            (wg.at[layer, :, ks], gate_w.at[slot]),
            (wu.at[layer, :, ks], up_w.at[slot]),
        )
        return [pltpu.make_async_copy(s, d, w_sem.at[slot, n]) for n, (s, d) in enumerate(pairs)]

    x_copy = pltpu.make_async_copy(x_hbm, x, x_sem)
    x_copy.start()
    for step in range(2):
        for copy in weights(step, step):
            copy.start()
    k_copy = pltpu.make_async_copy(kc.at[layer], keys, kv_sem.at[0])
    v_copy = pltpu.make_async_copy(vc.at[layer], vals, kv_sem.at[1])
    k_copy.start()
    v_copy.start()
    x_copy.wait()

    @pl.loop(0, rows // 32)
    def _(i):
        r = pl.ds(pl.multiple_of(i * 32, 32), 32)
        total = jnp.zeros((32, 128), F32)
        for c0 in range(0, x.shape[1], 128):
            v = x[r, c0:c0 + 128].astype(F32)
            total = total + v * v
        mean = jnp.sum(total, axis=-1, keepdims=True) / x.shape[1]
        inv_ref[r, :] = jnp.broadcast_to(lax.rsqrt(mean + NORM_EPS), (32, 128))

    @pl.loop(0, steps)
    def _(step):
        slot = lax.rem(step, 2)
        ks = pl.ds(pl.multiple_of(step * kb, kb), kb)
        g = gain[layer:layer + 1, ks]

        @pl.loop(0, rows // 32)
        def _(i):
            r = pl.ds(pl.multiple_of(i * 32, 32), 32)
            a[r, :] = (x[r, ks].astype(F32) * inv_ref[r, 0:1] * g).astype(BF)

        for copy in weights(step, slot):
            copy.wait()
        first = step == 0
        part = lax.dot_general(a[...], gate_w[slot], NT_DIMS, preferred_element_type=F32)
        gate[...] = jnp.where(first, 0.0, gate[...]) + part
        part = lax.dot_general(a[...], up_w[slot], NT_DIMS, preferred_element_type=F32)
        up[...] = jnp.where(first, 0.0, up[...]) + part
        part = jnp.dot(a[...], qkv_w[slot], preferred_element_type=F32)
        qkv[...] = jnp.where(first, 0.0, qkv[...]) + part

        @pl.when(step + 2 < steps)
        def _():
            for copy in weights(step + 2, slot):
                copy.start()

    @pl.loop(0, rows // 16)
    def _(i):
        r = pl.ds(pl.multiple_of(i * 16, 16), 16)
        g16 = gate[r, :].astype(BF).astype(F32)
        u16 = up[r, :].astype(BF).astype(F32)
        h_ref[r, qw:qw + ff] = (g16 * (1.0 / (1.0 + jnp.exp(-g16))) * u16).astype(BF)

    k_copy.wait()
    v_copy.wait()

    @pl.loop(0, rows // 32)
    def _(i):
        for half in range(2):
            t0 = pl.multiple_of(i * 32 + half * 16, 16)
            outs = [attend_block(pl.multiple_of(t0 + 8 * n, 8), qkv, cos, sin, bound, keys, vals, groups, head, seq) for n in range(2)]
            for h in range(groups):
                both = jnp.concatenate([outs[0][h], outs[1][h]], axis=0)
                h_ref[pl.ds(t0, 16), head * h:head * (h + 1)] = both.astype(BF)


def back_kernel(layer, dims, last, h_ref, x_hbm, wo, wd, out_ref, w, send_p, recv_p, own_p, send_i, recv_i, x_own, xg,
                w_sem, x_sem, pair_s, pair_r, ici_s, ici_r, ag_s, ag_r, fwd_s, fwd_r, out_sem):
    cw, qw = dims
    rows, ff = h_ref.shape[0], h_ref.shape[1] - qw
    half = rows // 2
    me = lax.axis_index("tp")
    core, chip = lax.rem(me, 2), me // 2
    mate = me + 1 - 2 * core
    chip_x = chip + 1 - 2 * lax.rem(chip, 2)
    chip_y = chip + 2 - 4 * (chip // 2)
    chip_d = 3 - chip
    order = (chip_d, chip_y, chip_x, chip)

    def cols(device):
        return pl.ds(pl.multiple_of(device * cw, cw), cw)

    def weights(step):
        slot, q = step % 2, order[step]
        copies = []
        for n, device in enumerate((2 * q + 1 - core, 2 * q + core)):
            for m, (src, r0, r1) in enumerate(((wo, 0, qw), (wd, qw, qw + ff))):
                copies.append(pltpu.make_async_copy(
                    src.at[layer, :, cols(device)], w.at[slot, r0:r1, n * cw:(n + 1) * cw], w_sem.at[slot, 2 * n + m]))
        return copies

    for step in range(2):
        for copy in weights(step):
            copy.start()
    x_copy = pltpu.make_async_copy(x_hbm.at[:, cols(me)], x_own, x_sem)
    x_copy.start()

    barrier = pltpu.get_barrier_semaphore()
    for device in (mate, 2 * chip_x + core, 2 * chip_y + core, 2 * chip_d + core):
        pl.semaphore_signal(barrier, inc=1, device_id={"tp": device}, device_id_type=MESH)
    pl.semaphore_wait(barrier, 4)

    def remote(src, dst, s_sem, r_sem, device):
        return pltpu.make_async_remote_copy(src_ref=src, dst_ref=dst, send_sem=s_sem, recv_sem=r_sem,
                                            device_id={"tp": device}, device_id_type=MESH)

    pair = [remote(send_p.at[i], recv_p.at[i], pair_s.at[i], pair_r.at[i], mate) for i in range(4)]
    ici = [remote(send_i.at[i], recv_i.at[i], ici_s.at[i], ici_r.at[i], 2 * order[i] + core) for i in range(3)]

    def settle(i):
        pair[i].wait_recv()
        if i < 3:
            @pl.loop(0, rows // 32)
            def _(n):
                r = pl.ds(pl.multiple_of(n * 32, 32), 32)
                send_i[i, r, :] = (own_p[i, r, :] + recv_p[i, r, :]).astype(BF)
            ici[i].start()

    for step in range(4):
        for copy in weights(step):
            copy.wait()
        part = jnp.dot(h_ref[...], w[step % 2], preferred_element_type=F32)
        send_p[step] = part[:, 0:cw]
        pair[step].start()
        own_p[step] = part[:, cw:2 * cw]
        if step + 2 < 4:
            for copy in weights(step + 2):
                copy.start()
        if step >= 1:
            settle(step - 1)
    settle(3)
    x_copy.wait()
    for i in range(3):
        ici[i].wait_recv()

    @pl.loop(0, rows // 32)
    def _(n):
        r = pl.ds(pl.multiple_of(n * 32, 32), 32)
        total = own_p[3, r, :] + recv_p[3, r, :]
        for i in range(3):
            total = total + recv_i[i, r, :].astype(F32)
        xg[r, cols(me)] = (x_own[r, :].astype(F32) + total).astype(BF)

    def share(r0, r1, owner, s_sem, r_sem, device):
        block = xg.at[r0:r1, cols(owner)]
        return remote(block, block, s_sem, r_sem, device)

    near = [share(0, rows, me, ag_s.at[n], ag_r.at[n], 2 * q + core) for n, q in enumerate((chip_x, chip_y))]
    for copy in near:
        copy.start()
    to_mate = [
        share(0, rows, me, fwd_s.at[0], fwd_r.at[0], mate),
        share(0, rows, 2 * chip_x + core, fwd_s.at[1], fwd_r.at[1], mate),
        share(0, rows, 2 * chip_y + core, fwd_s.at[2], fwd_r.at[2], mate),
        share(0, half, 2 * chip_d + core, fwd_s.at[3], fwd_r.at[3], mate),
        share(half, rows, 2 * chip_d + core, fwd_s.at[4], fwd_r.at[4], mate),
    ]
    far = [
        share(0, half, 2 * chip_x + core, ag_s.at[2], ag_r.at[2], 2 * chip_y + core),
        share(half, rows, 2 * chip_y + core, ag_s.at[3], ag_r.at[3], 2 * chip_x + core),
    ]
    to_mate[0].start()
    for n in range(2):
        near[n].wait_recv()
        far[n].start()
        to_mate[1 + n].start()
    for n in range(2):
        far[n].wait_recv()
        to_mate[3 + n].start()
    for copy in to_mate:
        copy.wait_recv()
    out = pltpu.make_async_copy(xg, out_ref, out_sem)
    out.start()
    for copy in pair + ici + near + far + to_mate:
        copy.wait_send()
    out.wait()


def solution(mesh):
    tp = mesh.shape["tp"]
    arg_specs = (P("dp", None), P("dp"), P(), P(None, None, "tp"), P(None, None, "tp"), P(None, None, "tp"), P(None, "tp", None), P(None, None, "tp"), P(None, None, "tp"), P(None, "tp", None), P(None, "dp", None, "tp", None), P(None, "dp", None, "tp", None))
    hbm = pl.BlockSpec(memory_space=pl.ANY)
    vmem = pl.BlockSpec(memory_space=pltpu.VMEM)
    dma = pltpu.SemaphoreType.DMA

    def per_device(x_in, lengths, norm_gain, w_q, w_k, w_v, w_o, w_gate, w_up, w_down, k_cache, v_cache):
        rows, width = x_in.shape
        layers, _, seq, _, head = k_cache.shape
        qw, ff = w_q.shape[-1], w_gate.shape[-1]
        groups = qw // head
        cw = width // tp
        kb = 2 * cw
        inv_freq = 1.0 / (ROPE_BASE ** (jnp.arange(0, head, 2).astype(F32) / head))
        angles = lengths.astype(F32)[:, None] * inv_freq[None, :]
        cos, sin = jnp.cos(angles), jnp.sin(angles)
        cos = jnp.concatenate([cos, cos], axis=1)
        sin = jnp.concatenate([-sin, sin], axis=1)
        bound = jnp.broadcast_to(lengths[:, None], (rows, 128))
        gain = norm_gain.astype(F32)
        gate_t, up_t = jnp.swapaxes(w_gate, 1, 2), jnp.swapaxes(w_up, 1, 2)
        kc = k_cache.reshape(layers, rows * seq, head)
        vc = v_cache.reshape(layers, rows * seq, head)
        x = x_in
        for layer in range(layers):
            h = pl.pallas_call(
                functools.partial(front_kernel, layer, (groups, head, seq, kb, width // kb)),
                out_shape=jax.ShapeDtypeStruct((rows, qw + ff), BF),
                in_specs=[hbm, vmem, vmem, vmem, vmem] + [hbm] * 7,
                out_specs=vmem,
                scratch_shapes=[
                    pltpu.VMEM((rows, width), BF), pltpu.VMEM((rows, kb), BF), pltpu.VMEM((rows, 128), F32),
                    pltpu.VMEM((2, kb, qw + 2 * head), BF), pltpu.VMEM((2, ff, kb), BF), pltpu.VMEM((2, ff, kb), BF),
                    pltpu.VMEM((rows, qw + 2 * head), F32), pltpu.VMEM((rows, ff), F32), pltpu.VMEM((rows, ff), F32),
                    pltpu.VMEM((rows * seq, head), BF), pltpu.VMEM((rows * seq, head), BF),
                    dma, dma((2, 5)), dma((2,)),
                ],
                compiler_params=pltpu.CompilerParams(vmem_limit_bytes=63 * 2**20),
                name=f"front{layer}",
            )(x, bound, cos, sin, gain, w_q, w_k, w_v, gate_t, up_t, kc, vc)
            x = pl.pallas_call(
                functools.partial(back_kernel, layer, (cw, qw), layer == layers - 1),
                out_shape=jax.ShapeDtypeStruct((rows, width), BF),
                in_specs=[vmem, hbm, hbm, hbm],
                out_specs=hbm,
                scratch_shapes=[
                    pltpu.VMEM((2, qw + ff, kb), BF),
                    pltpu.VMEM((4, rows, cw), F32), pltpu.VMEM((4, rows, cw), F32), pltpu.VMEM((4, rows, cw), F32),
                    pltpu.VMEM((3, rows, cw), BF), pltpu.VMEM((3, rows, cw), BF),
                    pltpu.VMEM((rows, cw), BF), pltpu.VMEM((rows, width), BF),
                    dma((2, 4)), dma, dma((4,)), dma((4,)), dma((3,)), dma((3,)),
                    dma((4,)), dma((4,)), dma((5,)), dma((5,)), dma,
                ],
                compiler_params=pltpu.CompilerParams(vmem_limit_bytes=60 * 2**20, collective_id=layer, has_side_effects=True),
                name=f"back{layer}",
            )(h, x, w_o, w_down)
        return x

    return jax.shard_map(per_device, mesh=mesh, in_specs=arg_specs, out_specs=P("dp", None), check_vma=False)
```

time: 444 us -> 299 us (0.67); the launches traced: 437 us -> 298 us
  Pallas kernels: 0 us -> 287 us
  matrix products: 166 us -> 0 us
  waiting for transfers between devices: 133 us -> 0 us
  blocking collectives: 62.8 us -> 0 us
  other arithmetic: 32.2 us -> 4.07 us
  local copies, waits for them, and re-layouts: 22.7 us -> 6.7 us
  between operations: 14.2 us -> 0.04 us
  starting transfers between devices: 5.71 us -> 0 us
    pallas_call x0 -> x4, Pallas kernels: none -> 287 us  [the longest x2 147 us: per_device(): pl.pallas_call(functools.partial(back_kernel, layer, (cw, qw), layer == l...]
    dot_general x18 -> x0, matrix products: 166 us -> none  [the longest x2 33.3 us: layer_update(): jnp.dot(normed, wu_layer, preferred_element_type=jnp.float32)]
    all_gather x2 -> x0, waiting for transfers between devices: 72.9 us -> none  [per_device(): x_res = lax.all_gather(new_cols, 'tp', axis=1, tiled=True)]
    all_to_all x1 -> x0, blocking collectives: 62.8 us -> none  [per_device(): received = lax.all_to_all(partial_sum, 'tp', 1, 0, tiled=True)]
    all_to_all x1 -> x0, waiting for transfers between devices: 60.4 us -> none  [per_device(): received = lax.all_to_all(partial_sum, 'tp', 1, 0, tiled=True)]
    reduce_sum x6 -> x0, other arithmetic: 16.2 us -> none  [the longest x2 7.32 us: rms_norm(): jnp.mean(x_f32 * x_f32, axis=-1, keepdims=True) + NORM_EPS]
    unnamed x31 -> x1, local copies, waits for them, and re-layouts: 13.1 us -> 5.18 us
    all_to_all x1 -> x0, starting transfers between devices: 5.46 us -> none  [per_device(): received = lax.all_to_all(partial_sum, 'tp', 1, 0, tiled=True)]
  transfers between devices with their start and end apart: 3 -> 0, of which waited for: 3 -> 0; matrix products, arithmetic and copies ran while one was open for 0% -> 0% of each run, Pallas kernels for 0% -> 0%
where the time goes in v1:
time: 299 us; the launch traced here: 298 us
  Pallas kernels  287 us (96%)
  local copies, waits for them, and re-layouts  6.7 us (2%)
  other arithmetic  4.07 us (1%)
    pallas_call x2, Pallas kernels, per_device(): pl.pallas_call(functools.partial(back_kernel, layer, (cw, qw), layer == l...  147 us
    pallas_call x2, Pallas kernels, per_device(): pl.pallas_call(functools.partial(front_kernel, layer, (groups, head, seq,...  140 us

profile of v1, /device:TPU:0, one launch (start us, length us, event | category | flops | bytes accessed | tf_op | source)
XLA Modules:
  0.0 298.0 jit_solution(8768669555222377805)
XLA Ops:
  0.0 0.7 convert_element_type.13
  0.7 1.3 convert_element_type.15.gain
  2.0 1.5 broadcast_in_dim.2.bound
  3.6 1.0 fusion
  4.6 1.0 pad_maximum_fusion
  5.6 69.9 %front0.1.h_ref = bf16[512,2368]{1,0:T(8,128)(2,1)} custom-call(bf16[512,5120]{1,0:T(8,128)(2,1)} %x_hbm.3, s32[512,128]{1,0:T(8,128)} %broadcast_in_dim.2.bound, f32[512,128]{1,0:T(8,128)} %get-tuple-element.8.cos, f32[512,128]{1,0:T(8,128)} %get-tuple-element.9.sin, f32[2,5120]{1,0:T(2,128)} %convert_element_type.15.gain, bf16[2,5120,640]{2,1,0:T(8,128)(2,1)} %wq.3, ...), custom_call_target="tpu_custom_call" | custom-call | tf_op jit(solution)/shard_map/front0/pallas_call | solution.py:269
  75.5 74.2 %back0.1.x_hbm = bf16[512,5120]{1,0:T(8,128)(2,1)} custom-call(bf16[512,2368]{1,0:T(8,128)(2,1)} %front0.1.h_ref, bf16[512,5120]{1,0:T(8,128)(2,1)} %x_hbm.3, bf16[2,640,5120]{2,1,0:T(8,128)(2,1)} %wo.3, bf16[2,1728,5120]{2,1,0:T(8,128)(2,1)} %wd.3), custom_call_target="tpu_custom_call" | custom-call | tf_op jit(solution)/shard_map/back0/pallas_call | solution.py:284
  149.8 70.3 %front1.1.h_ref = bf16[512,2368]{1,0:T(8,128)(2,1)} custom-call(bf16[512,5120]{1,0:T(8,128)(2,1)} %back0.1.x_hbm, s32[512,128]{1,0:T(8,128)} %broadcast_in_dim.2.bound, f32[512,128]{1,0:T(8,128)} %get-tuple-element.8.cos, f32[512,128]{1,0:T(8,128)} %get-tuple-element.9.sin, f32[2,5120]{1,0:T(2,128)} %convert_element_type.15.gain, bf16[2,5120,640]{2,1,0:T(8,128)(2,1)} %wq.3, ...), custom_call_target="tpu_custom_call" | custom-call | tf_op jit(solution)/shard_map/front1/pallas_call | solution.py:269
  220.1 72.7 %back1.1 = bf16[512,5120]{1,0:T(8,128)(2,1)} custom-call(bf16[512,2368]{1,0:T(8,128)(2,1)} %front1.1.h_ref, bf16[512,5120]{1,0:T(8,128)(2,1)} %back0.1.x_hbm, bf16[2,640,5120]{2,1,0:T(8,128)(2,1)} %wo.3, bf16[2,1728,5120]{2,1,0:T(8,128)(2,1)} %wd.3), custom_call_target="tpu_custom_call" | custom-call | tf_op jit(solution)/shard_map/back1/pallas_call | solution.py:284
  292.8 5.2 %copy.14 = bf16[512,5120]{1,0:T(8,128)(2,1)} copy(bf16[512,5120]{1,0:T(8,128)(2,1)} %back1.1) | data formatting | bytes 10485760
  (1 shorter events, 0.0 us)

commit v2 on v0

v2 whole, which is shorter than its diff:
```python
import functools

import jax
import jax.numpy as jnp
from jax import lax
from jax.experimental import pallas as pl
from jax.experimental.pallas import tpu as pltpu
from jax.sharding import PartitionSpec as P

NORM_EPS = 1e-5
ROPE_BASE = 500000.0
MESH = pl.DeviceIdType.MESH
BF, F32 = jnp.bfloat16, jnp.float32
PER = 2
NT_DIMS = (((1,), (1,)), ((), ()))


def attention(qkv, cos, sin, bound, keys, vals, h_ref, bufs, groups, head, seq):
    qb, ob, lb, pb, pob = bufs
    per = qb.shape[1]
    span = 8 * seq
    n_groups = qkv.shape[0] // (8 * per)
    scale = head ** -0.5
    col = lax.broadcasted_iota(jnp.int32, (8, span), 1)
    low = lax.broadcasted_iota(jnp.int32, (8, span), 0) * seq

    def start_of(g, n):
        return pl.multiple_of(g * (8 * per) + 8 * n, 8)

    def project(g):
        slot = lax.rem(g, 2)
        for n in range(per):
            rows = pl.ds(start_of(g, n), 8)
            c, s = cos[rows, :], sin[rows, :]

            def turn(j):
                v = qkv[rows, head * j:head * (j + 1)].astype(BF).astype(F32)
                return (v * c + pltpu.roll(v, head // 2, 1) * s).astype(BF).astype(F32)

            k_new = turn(groups)
            for j in range(groups):
                q = turn(j)
                qb[slot, n, 8 * j:8 * (j + 1), :] = q
                own = jnp.sum(q * k_new, axis=-1, keepdims=True) * scale
                ob[slot, n, 8 * j:8 * (j + 1), :] = jnp.broadcast_to(own, (8, 128))

    def score(g):
        slot = lax.rem(g, 2)
        for n in range(per):
            t0 = start_of(g, n)
            cached = pl.ds(pl.multiple_of(t0 * seq, span), span)
            logits = lax.dot_general(qb[slot, n].astype(BF), keys[cached, :], NT_DIMS, preferred_element_type=F32) * scale
            b = bound[pl.ds(t0, 8), :]
            high = jnp.concatenate([b] * (span // 128), axis=1) + low
            keep = (col >= low) & (col < high)
            for j in range(groups):
                lb[slot, n, 8 * j:8 * (j + 1), :] = jnp.where(keep, logits[8 * j:8 * (j + 1)], -jnp.inf)

    def weigh(g):
        slot = lax.rem(g, 2)
        for n in range(per):
            for j in range(groups):
                r = slice(8 * j, 8 * (j + 1))
                logits, own = lb[slot, n, r, :], ob[slot, n, r, :]
                peak = jnp.maximum(jnp.max(logits, axis=-1, keepdims=True), own)
                w = [jnp.exp(logits[:, c0:c0 + 128] - peak) for c0 in range(0, span, 128)]
                w_own = jnp.exp(own - peak)
                inv = 1.0 / (jnp.sum(sum(w[1:], w[0]), axis=-1, keepdims=True) + w_own)
                for m, v in enumerate(w):
                    pb[slot, n, r, 128 * m:128 * (m + 1)] = v * inv
                pob[slot, n, r, :] = (w_own * inv).astype(BF).astype(F32)

    def mix(g):
        slot = lax.rem(g, 2)
        for n0 in range(0, per, 2):
            outs = []
            for n in (n0, n0 + 1):
                t0 = start_of(g, n)
                cached = pl.ds(pl.multiple_of(t0 * seq, span), span)
                out = jnp.dot(pb[slot, n].astype(BF), vals[cached, :], preferred_element_type=F32)
                v_new = qkv[pl.ds(t0, 8), (groups + 1) * head:].astype(BF).astype(F32)
                outs.append([out[8 * j:8 * (j + 1)] + pob[slot, n, 8 * j:8 * (j + 1), :] * v_new for j in range(groups)])
            for j in range(groups):
                both = jnp.concatenate([outs[0][j], outs[1][j]], axis=0).astype(BF)
                h_ref[pl.ds(pl.multiple_of(start_of(g, n0), 16), 16), head * j:head * (j + 1)] = both

    @pl.loop(0, n_groups + 3)
    def _(i):
        for lag, stage in ((3, mix), (2, weigh), (1, score), (0, project)):
            stage(jnp.clip(i - lag, 0, n_groups - 1))


def place(core, chip, fx, fy):
    x, y = lax.rem(chip, 2), chip // 2
    return 2 * (y + fy * (1 - 2 * y)) + (x + fx * (1 - 2 * x))


def remote(src, dst, send_sem, recv_sem, device):
    return pltpu.make_async_remote_copy(src_ref=src, dst_ref=dst, send_sem=send_sem, recv_sem=recv_sem,
                                        device_id={"tp": device}, device_id_type=MESH)


def columns(device, width):
    return pl.ds(pl.multiple_of(device * width, width), width)


def gather_plan(me, xg, cw, send_sem, recv_sem):
    core, chip = lax.rem(me, 2), me // 2
    mate = me + 1 - 2 * core
    first = 2 * place(core, chip, 1 - core, core) + core
    second = 2 * place(core, chip, core, 1 - core) + core
    across = 2 * (3 - chip) + core
    rows = xg.shape[0]
    half = rows // 2

    def share(n, r0, r1, owner, device):
        block = xg.at[r0:r1, columns(owner, cw)]
        return remote(block, block, send_sem.at[n], recv_sem.at[n], device)

    near = [share(0, 0, rows, me, first), share(1, 0, rows, me, second)]
    far = [share(2, 0, half, first, second), share(3, half, rows, second, first)]
    to_mate = [share(4, 0, rows, me, mate), share(5, 0, rows, first, mate), share(6, 0, rows, second, mate),
               share(7, 0, half, across, mate), share(8, half, rows, across, mate)]
    return near, far, to_mate


def greet(me, peers):
    barrier = pltpu.get_barrier_semaphore()
    for device in peers:
        pl.semaphore_signal(barrier, inc=1, device_id={"tp": device}, device_id_type=MESH)
    pl.semaphore_wait(barrier, len(peers))


def front_kernel(layer, dims, gathered, x_hbm, bound, cos, sin, gain, wq, wk, wv, wg, wu, kc, vc, h_ref,
                 x, a, inv_ref, qkv_w, gate_w, up_w, qkv, gate, up, keys, vals, qb, ob, lb, pb, pob, x_sem, w_sem, kv_sem,
                 sums=None, sum_s=None, sum_r=None, ag_s=None, ag_r=None):
    groups, head, seq, kb, steps = dims
    qw = groups * head
    rows, width = x.shape
    ff = gate.shape[1]
    cw = kb // 2
    if gathered:
        me = lax.axis_index("tp")
        core, chip = lax.rem(me, 2), me // 2
    else:
        core, chip = 0, 0

    def sources(step):
        moved, both = (step + 2) // 3, step // 3
        swap = step // 2 * (1 - lax.rem(step, 2))
        return 2 * place(core, chip, moved, both) + swap, 2 * place(core, chip, both, moved) + 1 - swap

    def weights(step, slot):
        groups_of = ([], [], [])
        for part, device in enumerate(sources(step)):
            ks, to = columns(device, cw), slice(part * cw, (part + 1) * cw)
            pairs = (
                (0, wq.at[layer, ks, :], qkv_w.at[slot, to, 0:qw]),
                (0, wk.at[layer, ks, :], qkv_w.at[slot, to, qw:qw + head]),
                (0, wv.at[layer, ks, :], qkv_w.at[slot, to, qw + head:qw + 2 * head]),
                (1, wg.at[layer, :, ks], gate_w.at[slot, :, to]),
                (2, wu.at[layer, :, ks], up_w.at[slot, :, to]),
            )
            for n, (which, src, dst) in enumerate(pairs):
                groups_of[which].append(pltpu.make_async_copy(src, dst, w_sem.at[slot, part * 5 + n]))
        return groups_of

    def start_weights(step, slot):
        for group in weights(step, slot):
            for copy in group:
                copy.start()

    kv = [pltpu.make_async_copy(kc.at[layer], keys, kv_sem.at[0]), pltpu.make_async_copy(vc.at[layer], vals, kv_sem.at[1])]
    if gathered:
        x_copy = pltpu.make_async_copy(x_hbm, x.at[:, columns(me, cw)], x_sem)
        x_copy.start()
        start_weights(0, 0)
        near, far, to_mate = gather_plan(me, x, cw, ag_s, ag_r)
        peers = [lax.rem(me + n, 8) for n in range(1, 8)]
        greet(me, peers)
        x_copy.wait()
        for c0 in range(0, rows, 128):
            total = jnp.zeros((128, 128), F32)
            for n in range(cw // 128):
                v = x[c0:c0 + 128, pl.ds(pl.multiple_of(me * cw + n * 128, 128), 128)].astype(F32)
                total = total + v * v
            by_row = jnp.broadcast_to(jnp.sum(total, axis=-1, keepdims=True), (128, 128))
            sums[me, :, c0:c0 + 128] = by_row.T[0:8]
        swap_sums = [remote(sums.at[me], sums.at[me], sum_s.at[n], sum_r.at[n], peer) for n, peer in enumerate(peers)]
        for copy in swap_sums + near + to_mate[:1]:
            copy.start()
        for n, copy in enumerate(swap_sums):
            sender = lax.rem(me + 7 - n, 8)
            remote(sums.at[sender], sums.at[sender], sum_s.at[n], sum_r.at[n], sender).wait_recv()
        for c0 in range(0, rows, 128):
            total = sums[0, :, c0:c0 + 128]
            for n in range(1, 8):
                total = total + sums[n, :, c0:c0 + 128]
            inv = lax.rsqrt(total / width + NORM_EPS)
            inv_ref[c0:c0 + 128, :] = jnp.broadcast_to(inv[0:1], (128, 128)).T
    else:
        x_copy = pltpu.make_async_copy(x_hbm, x, x_sem)
        x_copy.start()
        start_weights(0, 0)
        x_copy.wait()

        @pl.loop(0, rows // 128)
        def _(i):
            r = pl.ds(pl.multiple_of(i * 128, 128), 128)
            total = jnp.zeros((128, 128), F32)
            for c0 in range(0, width, 128):
                v = x[r, c0:c0 + 128].astype(F32)
                total = total + v * v
            mean = jnp.sum(total, axis=-1, keepdims=True) / width
            inv_ref[r, :] = jnp.broadcast_to(lax.rsqrt(mean + NORM_EPS), (128, 128))

    @pl.loop(0, steps)
    def _(step):
        slot = lax.rem(step, 2)
        if gathered:
            for n in range(3):
                @pl.when(step == n)
                def _(n=n):
                    to_mate[n].wait_recv()

            @pl.when(step == 3)
            def _():
                to_mate[3].wait_recv()
                to_mate[4].wait_recv()

        devices = sources(step)

        @pl.loop(0, rows // 64)
        def _(i):
            r = pl.ds(pl.multiple_of(i * 64, 64), 64)
            inv = inv_ref[r, :]
            for part, device in enumerate(devices):
                for c0 in range(0, cw, 128):
                    cs = pl.ds(pl.multiple_of(device * cw + c0, 128), 128)
                    a[r, part * cw + c0:part * cw + c0 + 128] = (x[r, cs].astype(F32) * inv * gain[layer:layer + 1, cs]).astype(BF)

        first = step == 0
        w_copies = weights(step, slot)
        for copy in w_copies[0]:
            copy.wait()
        part = jnp.dot(a[...], qkv_w[slot], preferred_element_type=F32)
        qkv[...] = jnp.where(first, 0.0, qkv[...]) + part
        for copy in w_copies[1]:
            copy.wait()

        @pl.when(step + 1 < steps)
        def _():
            start_weights(step + 1, 1 - slot)

        @pl.when(step == steps - 1)
        def _():
            for copy in kv:
                copy.start()

        part = lax.dot_general(a[...], gate_w[slot], NT_DIMS, preferred_element_type=F32)
        gate[...] = jnp.where(first, 0.0, gate[...]) + part
        if gathered:
            @pl.when(step == 0)
            def _():
                near[0].wait_recv()
                to_mate[1].start()
                far[0].start()
        for copy in w_copies[2]:
            copy.wait()
        part = lax.dot_general(a[...], up_w[slot], NT_DIMS, preferred_element_type=F32)
        up[...] = jnp.where(first, 0.0, up[...]) + part
        if gathered:
            @pl.when(step == 1)
            def _():
                near[1].wait_recv()
                to_mate[2].start()
                far[1].start()

            @pl.when(step == 2)
            def _():
                far[0].wait_recv()
                to_mate[3].start()
                far[1].wait_recv()
                to_mate[4].start()

    if gathered:
        for copy in swap_sums + near + far + to_mate:
            copy.wait_send()

    @pl.loop(0, rows // 32)
    def _(i):
        r = pl.ds(pl.multiple_of(i * 32, 32), 32)
        g_in = gate[r, :].astype(BF).astype(F32)
        u_in = up[r, :].astype(BF).astype(F32)
        h_ref[r, qw:qw + ff] = (g_in * (1.0 / (1.0 + jnp.exp(-g_in))) * u_in).astype(BF)

    for copy in kv:
        copy.wait()
    attention(qkv, cos, sin, bound, keys, vals, h_ref, (qb, ob, lb, pb, pob), groups, head, seq)


def front_call(layer, dims, rows, width, qw, ff, name, gathered=False):
    groups, head, seq, kb, _ = dims
    hbm = pl.BlockSpec(memory_space=pl.ANY)
    vmem = pl.BlockSpec(memory_space=pltpu.VMEM)
    dma = pltpu.SemaphoreType.DMA
    lanes = groups * 8
    return pl.pallas_call(
        functools.partial(front_kernel, layer, dims, gathered),
        out_shape=jax.ShapeDtypeStruct((rows, qw + ff), BF),
        in_specs=[hbm, vmem, vmem, vmem, vmem] + [hbm] * 7,
        out_specs=vmem,
        scratch_shapes=[
            pltpu.VMEM((rows, width), BF), pltpu.VMEM((rows, kb), BF), pltpu.VMEM((rows, 128), F32),
            pltpu.VMEM((2, kb, qw + 2 * head), BF), pltpu.VMEM((2, ff, kb), BF), pltpu.VMEM((2, ff, kb), BF),
            pltpu.VMEM((rows, qw + 2 * head), F32), pltpu.VMEM((rows, ff), F32), pltpu.VMEM((rows, ff), F32),
            pltpu.VMEM((rows * seq, head), BF), pltpu.VMEM((rows * seq, head), BF),
            pltpu.VMEM((2, PER, lanes, head), F32), pltpu.VMEM((2, PER, lanes, 128), F32),
            pltpu.VMEM((2, PER, lanes, 8 * seq), F32), pltpu.VMEM((2, PER, lanes, 8 * seq), F32),
            pltpu.VMEM((2, PER, lanes, 128), F32),
            dma, dma((2, 10)), dma((2,)),
        ] + ([pltpu.VMEM((8, 8, rows), F32), dma((7,)), dma((7,)), dma((9,)), dma((9,))] if gathered else []),
        compiler_params=pltpu.CompilerParams(vmem_limit_bytes=63 * 2**20, **({"collective_id": 2, "has_side_effects": True} if gathered else {})),
        name=name,
    )


UNITS = ((0, 0, 256), (0, 256, 640), (1, 0, 640), (2, 0, 640), (3, 0, 640))


def back_kernel(layer, dims, last, h_hbm, x_hbm, wo, wd, out_ref, h, w, send_p, recv_p, own_p, send_i, recv_i, x_own,
                h_sem, w_sem, x_sem, pair_s, pair_r, ici_s, ici_r, xg=None, ag_s=None, ag_r=None, out_sem=None):
    cw, qw = dims
    rows, ff = h.shape[0], h.shape[1] - qw
    me = lax.axis_index("tp")
    core, chip = lax.rem(me, 2), me // 2
    mate = me + 1 - 2 * core
    order = (place(core, chip, 1, 1), place(core, chip, 0, 1), place(core, chip, 1, 0), chip)
    n_units = len(UNITS)

    def weights(u):
        i, c0, c1 = UNITS[u]
        copies = []
        for n, device in enumerate((2 * order[i] + 1 - core, 2 * order[i] + core)):
            at = 2 * c0 + n * (c1 - c0)
            for m, (src, r0, r1) in enumerate(((wo, 0, qw), (wd, qw, qw + ff))):
                copies.append(pltpu.make_async_copy(
                    src.at[layer, :, pl.ds(pl.multiple_of(device * cw + c0, 128), c1 - c0)],
                    w.at[i % 2, r0:r1, at:at + c1 - c0], w_sem.at[u, 2 * n + m]))
        return copies

    h_copy = pltpu.make_async_copy(h_hbm, h, h_sem)
    h_copy.start()
    for u in range(3):
        for copy in weights(u):
            copy.start()
    x_copy = pltpu.make_async_copy(x_hbm if x_hbm.shape[1] == cw else x_hbm.at[:, columns(me, cw)], x_own, x_sem)
    x_copy.start()
    greet(me, [mate] + [2 * q + core for q in order[:3]])

    pair, ici = [], []
    for u, (i, c0, c1) in enumerate(UNITS):
        pair.append(remote(send_p.at[i, :, c0:c1], recv_p.at[i, :, c0:c1], pair_s.at[u], pair_r.at[u], mate))
        if i < 3:
            ici.append(remote(send_i.at[i, :, c0:c1], recv_i.at[i, :, c0:c1], ici_s.at[u], ici_r.at[u], 2 * order[i] + core))

    def settle(u):
        i, c0, c1 = UNITS[u]
        pair[u].wait_recv()
        if i < 3:
            @pl.loop(0, rows // 64)
            def _(n):
                r = pl.ds(pl.multiple_of(n * 64, 64), 64)
                send_i[i, r, c0:c1] = (own_p[i, r, c0:c1] + recv_p[i, r, c0:c1]).astype(BF)
            ici[u].start()

    h_copy.wait()
    for u, (i, c0, c1) in enumerate(UNITS):
        for copy in weights(u):
            copy.wait()
        part = jnp.dot(h[...], w[i % 2, :, 2 * c0:2 * c1], preferred_element_type=F32)
        send_p[i, :, c0:c1] = part[:, 0:c1 - c0]
        pair[u].start()
        own_p[i, :, c0:c1] = part[:, c1 - c0:]
        if u == n_units - 1 or UNITS[u + 1][0] != i:
            for v in range(n_units):
                if UNITS[v][0] == i + 2:
                    for copy in weights(v):
                        copy.start()
        if u >= 1:
            settle(u - 1)
    settle(n_units - 1)
    x_copy.wait()
    for copy in ici:
        copy.wait_recv()

    @pl.loop(0, rows // 64)
    def _(n):
        r = pl.ds(pl.multiple_of(n * 64, 64), 64)
        total = own_p[3, r, :] + recv_p[3, r, :]
        for i in range(3):
            total = total + recv_i[i, r, :].astype(F32)
        new = (x_own[r, :].astype(F32) + total).astype(BF)
        if last:
            xg[r, columns(me, cw)] = new
        else:
            out_ref[r, :] = new

    if last:
        near, far, to_mate = gather_plan(me, xg, cw, ag_s, ag_r)
        for copy in near + to_mate[:1]:
            copy.start()
        for n in range(2):
            near[n].wait_recv()
            far[n].start()
            to_mate[1 + n].start()
        for n in range(2):
            far[n].wait_recv()
            to_mate[3 + n].start()
        for copy in to_mate:
            copy.wait_recv()
        out = pltpu.make_async_copy(xg, out_ref, out_sem)
        out.start()
        for copy in near + far + to_mate:
            copy.wait_send()
        out.wait()
    for copy in pair + ici:
        copy.wait_send()


def back_call(layer, name, cid, last=True, rows=512, width=5120, cw=640, qw=640, ff=1728):
    hbm = pl.BlockSpec(memory_space=pl.ANY)
    dma = pltpu.SemaphoreType.DMA
    n = len(UNITS)
    return pl.pallas_call(
        functools.partial(back_kernel, layer, (cw, qw), last),
        out_shape=jax.ShapeDtypeStruct((rows, width if last else cw), BF),
        in_specs=[hbm, hbm, hbm, hbm],
        out_specs=hbm if last else pl.BlockSpec(memory_space=pltpu.VMEM),
        scratch_shapes=[
            pltpu.VMEM((rows, qw + ff), BF), pltpu.VMEM((2, qw + ff, 2 * cw), BF),
            pltpu.VMEM((4, rows, cw), F32), pltpu.VMEM((4, rows, cw), F32), pltpu.VMEM((4, rows, cw), F32),
            pltpu.VMEM((3, rows, cw), BF), pltpu.VMEM((3, rows, cw), BF), pltpu.VMEM((rows, cw), BF),
            dma, dma((n, 4)), dma, dma((n,)), dma((n,)), dma((n,)), dma((n,)),
        ] + ([pltpu.VMEM((rows, width), BF), dma((9,)), dma((9,)), dma] if last else []),
        compiler_params=pltpu.CompilerParams(vmem_limit_bytes=60 * 2**20, collective_id=cid, has_side_effects=True),
        name=name,
    )


def solution(mesh):
    tp = mesh.shape["tp"]
    arg_specs = (P("dp", None), P("dp"), P(), P(None, None, "tp"), P(None, None, "tp"), P(None, None, "tp"), P(None, "tp", None), P(None, None, "tp"), P(None, None, "tp"), P(None, "tp", None), P(None, "dp", None, "tp", None), P(None, "dp", None, "tp", None))

    def per_device(x_in, lengths, norm_gain, w_q, w_k, w_v, w_o, w_gate, w_up, w_down, k_cache, v_cache):
        rows, width = x_in.shape
        layers, _, seq, _, head = k_cache.shape
        qw, ff = w_q.shape[-1], w_gate.shape[-1]
        groups = qw // head
        cw = width // tp
        kb = 2 * cw
        inv_freq = 1.0 / (ROPE_BASE ** (jnp.arange(0, head, 2).astype(F32) / head))
        angles = lengths.astype(F32)[:, None] * inv_freq[None, :]
        cos, sin = jnp.cos(angles), jnp.sin(angles)
        cos = jnp.concatenate([cos, cos], axis=1)
        sin = jnp.concatenate([-sin, sin], axis=1)
        bound = jnp.broadcast_to(lengths[:, None], (rows, 128))
        gain = norm_gain.astype(F32)
        gate_t, up_t = jnp.swapaxes(w_gate, 1, 2), jnp.swapaxes(w_up, 1, 2)
        kc = k_cache.reshape(layers, rows * seq, head)
        vc = v_cache.reshape(layers, rows * seq, head)
        x = x_in
        for layer in range(layers):
            last = layer == layers - 1
            dims = (groups, head, seq, kb, width // kb)
            h = front_call(layer, dims, rows, width, qw, ff, f"front{layer}", layer > 0)(
                x, bound, cos, sin, gain, w_q, w_k, w_v, gate_t, up_t, kc, vc)
            x = back_call(layer, f"back{layer}", layer, last, rows, width, cw, qw, ff)(h, x, w_o, w_down)
        return x

    return jax.shard_map(per_device, mesh=mesh, in_specs=arg_specs, out_specs=P("dp", None), check_vma=False)
```

time: 444 us -> 245 us (0.55); the launches traced: 437 us -> 243 us
  Pallas kernels: 0 us -> 233 us
  matrix products: 166 us -> 0 us
  waiting for transfers between devices: 133 us -> 0 us
  blocking collectives: 62.8 us -> 0 us
  other arithmetic: 32.2 us -> 4.04 us
  local copies, waits for them, and re-layouts: 22.7 us -> 6.68 us
  between operations: 14.2 us -> 0.04 us
  starting transfers between devices: 5.71 us -> 0 us
    pallas_call x0 -> x4, Pallas kernels: none -> 233 us  [the longest x2 120 us: per_device(): front_call(layer, dims, rows, width, qw, ff, f'front{layer}', layer > 0)]
    dot_general x18 -> x0, matrix products: 166 us -> none  [the longest x2 33.3 us: layer_update(): jnp.dot(normed, wu_layer, preferred_element_type=jnp.float32)]
    all_gather x2 -> x0, waiting for transfers between devices: 72.9 us -> none  [per_device(): x_res = lax.all_gather(new_cols, 'tp', axis=1, tiled=True)]
    all_to_all x1 -> x0, blocking collectives: 62.8 us -> none  [per_device(): received = lax.all_to_all(partial_sum, 'tp', 1, 0, tiled=True)]
    all_to_all x1 -> x0, waiting for transfers between devices: 60.4 us -> none  [per_device(): received = lax.all_to_all(partial_sum, 'tp', 1, 0, tiled=True)]
    reduce_sum x6 -> x0, other arithmetic: 16.2 us -> none  [the longest x2 7.32 us: rms_norm(): jnp.mean(x_f32 * x_f32, axis=-1, keepdims=True) + NORM_EPS]
    unnamed x31 -> x1, local copies, waits for them, and re-layouts: 13.1 us -> 5.18 us
    all_to_all x1 -> x0, starting transfers between devices: 5.46 us -> none  [per_device(): received = lax.all_to_all(partial_sum, 'tp', 1, 0, tiled=True)]
  transfers between devices with their start and end apart: 3 -> 0, of which waited for: 3 -> 0; matrix products, arithmetic and copies ran while one was open for 0% -> 0% of each run, Pallas kernels for 0% -> 0%
where the time goes in v2:
time: 245 us; the launch traced here: 243 us
  Pallas kernels  233 us (95%)
  local copies, waits for them, and re-layouts  6.68 us (3%)
  other arithmetic  4.04 us (2%)
    pallas_call x2, Pallas kernels, per_device(): front_call(layer, dims, rows, width, qw, ff, f'front{layer}', layer > 0)  120 us
    pallas_call x2, Pallas kernels, per_device(): back_call(layer, f'back{layer}', layer, last, rows, width, cw, qw, ff)  113 us
    unnamed x1, local copies, waits for them, and re-layouts  5.18 us

profile of v2, /device:TPU:0, one launch (start us, length us, event | category | flops | bytes accessed | tf_op | source)
XLA Modules:
  0.0 243.4 jit_solution(6537142057454471156)
XLA Ops:
  0.0 0.7 convert_element_type.13
  0.7 1.4 convert_element_type.15.gain
  2.1 1.5 broadcast_in_dim.2.bound
  3.6 1.0 fusion
  4.6 1.0 pad_maximum_fusion
  5.5 52.6 %front0.1.h_hbm = bf16[512,2368]{1,0:T(8,128)(2,1)} custom-call(bf16[512,5120]{1,0:T(8,128)(2,1)} %x_hbm.3, s32[512,128]{1,0:T(8,128)} %broadcast_in_dim.2.bound, f32[512,128]{1,0:T(8,128)} %get-tuple-element.8.cos, f32[512,128]{1,0:T(8,128)} %get-tuple-element.9.sin, f32[2,5120]{1,0:T(2,128)} %convert_element_type.15.gain, bf16[2,5120,640]{2,1,0:T(8,128)(2,1)} %wq.3, ...), custom_call_target="tpu_custom_call" | custom-call | tf_op jit(solution)/shard_map/front0/pallas_call | solution.py:476
  58.1 44.6 %back0.1.x_hbm = bf16[512,640]{1,0:T(8,128)(2,1)} custom-call(bf16[512,2368]{1,0:T(8,128)(2,1)} %front0.1.h_hbm, bf16[512,5120]{1,0:T(8,128)(2,1)} %x_hbm.3, bf16[2,640,5120]{2,1,0:T(8,128)(2,1)} %wo.3, bf16[2,1728,5120]{2,1,0:T(8,128)(2,1)} %wd.3), custom_call_target="tpu_custom_call" | custom-call | tf_op jit(solution)/shard_map/back0/pallas_call | solution.py:478
  102.8 67.4 %front1.1.h_hbm = bf16[512,2368]{1,0:T(8,128)(2,1)} custom-call(bf16[512,640]{1,0:T(8,128)(2,1)} %back0.1.x_hbm, s32[512,128]{1,0:T(8,128)} %broadcast_in_dim.2.bound, f32[512,128]{1,0:T(8,128)} %get-tuple-element.8.cos, f32[512,128]{1,0:T(8,128)} %get-tuple-element.9.sin, f32[2,5120]{1,0:T(2,128)} %convert_element_type.15.gain, bf16[2,5120,640]{2,1,0:T(8,128)(2,1)} %wq.3, ...), custom_call_target="tpu_custom_call" | custom-call | tf_op jit(solution)/shard_map/front1/pallas_call | solution.py:476
  170.2 68.1 %back1.1 = bf16[512,5120]{1,0:T(8,128)(2,1)} custom-call(bf16[512,2368]{1,0:T(8,128)(2,1)} %front1.1.h_hbm, bf16[512,640]{1,0:T(8,128)(2,1)} %back0.1.x_hbm, bf16[2,640,5120]{2,1,0:T(8,128)(2,1)} %wo.3, bf16[2,1728,5120]{2,1,0:T(8,128)(2,1)} %wd.3), custom_call_target="tpu_custom_call" | custom-call | tf_op jit(solution)/shard_map/back1/pallas_call | solution.py:478
  238.3 5.2 %copy.14 = bf16[512,5120]{1,0:T(8,128)(2,1)} copy(bf16[512,5120]{1,0:T(8,128)(2,1)} %back1.1) | data formatting | bytes 10485760
  (1 shorter events, 0.0 us)

commit v3 on v2

--- a/solution.py
+++ b/solution.py
@@ -2,6 +2,7 @@
 
 import jax
 import jax.numpy as jnp
+import numpy as np
 from jax import lax
 from jax.experimental import pallas as pl
 from jax.experimental.pallas import tpu as pltpu
@@ -11,82 +12,97 @@
 ROPE_BASE = 500000.0
 MESH = pl.DeviceIdType.MESH
 BF, F32 = jnp.bfloat16, jnp.float32
-PER = 2
+PER = 4
 NT_DIMS = (((1,), (1,)), ((), ()))
 
 
-def attention(qkv, cos, sin, bound, keys, vals, h_ref, bufs, groups, head, seq):
-    qb, ob, lb, pb, pob = bufs
-    per = qb.shape[1]
+def angle_table(seq, head):
+    freq = np.float32(1.0) / np.power(np.float32(ROPE_BASE), np.arange(0, head, 2, dtype=np.float32) / np.float32(head))
+    angle = np.arange(seq, dtype=np.float32)[:, None] * freq[None, :]
+    cos, sin = np.cos(angle.astype(np.float64)), np.sin(angle.astype(np.float64))
+    table = np.zeros((128, 2 * head), np.float32)
+    table[:seq] = np.concatenate([cos, cos, -sin, sin], axis=1)
+    return table
+
+
+def rotate(qkv, lens, table, groups, head):
+    at = lax.broadcasted_iota(jnp.int32, (head, head), 0)
+    to = lax.broadcasted_iota(jnp.int32, (head, head), 1)
+    swap = (at == lax.rem(to + head // 2, head)).astype(BF)
+
+    @pl.loop(0, qkv.shape[0] // 128)
+    def _(i):
+        r = pl.ds(pl.multiple_of(i * 128, 128), 128)
+        spot = lax.broadcasted_iota(jnp.int32, (128, 128), 1).astype(F32)
+        hot = (lens[r, :] == spot).astype(F32)
+        angle = jnp.dot(hot, table[...], precision=lax.Precision.HIGHEST, preferred_element_type=F32)
+        c, s = angle[:, 0:head], angle[:, head:2 * head]
+        for j in range(groups + 1):
+            v = qkv[r, head * j:head * (j + 1)].astype(BF)
+            other = jnp.dot(v, swap, preferred_element_type=F32)
+            qkv[r, head * j:head * (j + 1)] = v.astype(F32) * c + other * s
+
+
+def attention(qkv, lens, keys, vals, h_ref, bufs, groups, head, seq):
+    lb, pb = bufs
+    per = lb.shape[1]
     span = 8 * seq
     n_groups = qkv.shape[0] // (8 * per)
     scale = head ** -0.5
-    col = lax.broadcasted_iota(jnp.int32, (8, span), 1)
-    low = lax.broadcasted_iota(jnp.int32, (8, span), 0) * seq
-
-    def start_of(g, n):
-        return pl.multiple_of(g * (8 * per) + 8 * n, 8)
-
-    def project(g):
-        slot = lax.rem(g, 2)
-        for n in range(per):
-            rows = pl.ds(start_of(g, n), 8)
-            c, s = cos[rows, :], sin[rows, :]
-
-            def turn(j):
-                v = qkv[rows, head * j:head * (j + 1)].astype(BF).astype(F32)
-                return (v * c + pltpu.roll(v, head // 2, 1) * s).astype(BF).astype(F32)
-
-            k_new = turn(groups)
-            for j in range(groups):
-                q = turn(j)
-                qb[slot, n, 8 * j:8 * (j + 1), :] = q
-                own = jnp.sum(q * k_new, axis=-1, keepdims=True) * scale
-                ob[slot, n, 8 * j:8 * (j + 1), :] = jnp.broadcast_to(own, (8, 128))
+    col = lax.broadcasted_iota(jnp.int32, (8, span), 1).astype(F32)
+    low = (lax.broadcasted_iota(jnp.int32, (8, span), 0) * seq).astype(F32)
+    own = lax.broadcasted_iota(jnp.int32, (8, 128), 0) == lax.broadcasted_iota(jnp.int32, (8, 128), 1)
+    none = jnp.zeros((120, head), BF)
+
+    def block(g, n):
+        t0 = pl.multiple_of(g * (8 * per) + 8 * n, 8)
+        return t0, pl.ds(t0, 8), pl.ds(pl.multiple_of(t0 * seq, span), span)
 
     def score(g):
         slot = lax.rem(g, 2)
         for n in range(per):
-            t0 = start_of(g, n)
-            cached = pl.ds(pl.multiple_of(t0 * seq, span), span)
-            logits = lax.dot_general(qb[slot, n].astype(BF), keys[cached, :], NT_DIMS, preferred_element_type=F32) * scale
-            b = bound[pl.ds(t0, 8), :]
-            high = jnp.concatenate([b] * (span // 128), axis=1) + low
+            t0, rows, cached = block(g, n)
+            q = jnp.concatenate([qkv[rows, head * j:head * (j + 1)] for j in range(groups)], axis=0).astype(BF)
+            k_new = jnp.concatenate([qkv[rows, groups * head:(groups + 1) * head].astype(BF), none], axis=0)
+            old = lax.dot_general(q, keys[cached, :], NT_DIMS, preferred_element_type=F32) * scale
+            new = lax.dot_general(q, k_new, NT_DIMS, preferred_element_type=F32) * scale
+            high = jnp.concatenate([lens[rows, :]] * (span // 128), axis=1) + low
             keep = (col >= low) & (col < high)
             for j in range(groups):
-                lb[slot, n, 8 * j:8 * (j + 1), :] = jnp.where(keep, logits[8 * j:8 * (j + 1)], -jnp.inf)
+                r = slice(8 * j, 8 * (j + 1))
+                lb[slot, n, r, 0:span] = jnp.where(keep, old[r], -jnp.inf)
+                lb[slot, n, r, span:] = jnp.where(own, new[r], -jnp.inf)
 
     def weigh(g):
         slot = lax.rem(g, 2)
         for n in range(per):
             for j in range(groups):
                 r = slice(8 * j, 8 * (j + 1))
-                logits, own = lb[slot, n, r, :], ob[slot, n, r, :]
-                peak = jnp.maximum(jnp.max(logits, axis=-1, keepdims=True), own)
-                w = [jnp.exp(logits[:, c0:c0 + 128] - peak) for c0 in range(0, span, 128)]
-                w_own = jnp.exp(own - peak)
-                inv = 1.0 / (jnp.sum(sum(w[1:], w[0]), axis=-1, keepdims=True) + w_own)
+                logits = [lb[slot, n, r, c0:c0 + 128] for c0 in range(0, span + 128, 128)]
+                peak = jnp.max(functools.reduce(jnp.maximum, logits), axis=-1, keepdims=True)
+                w = [jnp.exp(v - peak) for v in logits]
+                inv = 1.0 / jnp.sum(functools.reduce(jnp.add, w), axis=-1, keepdims=True)
                 for m, v in enumerate(w):
                     pb[slot, n, r, 128 * m:128 * (m + 1)] = v * inv
-                pob[slot, n, r, :] = (w_own * inv).astype(BF).astype(F32)
 
     def mix(g):
         slot = lax.rem(g, 2)
         for n0 in range(0, per, 2):
             outs = []
             for n in (n0, n0 + 1):
-                t0 = start_of(g, n)
-                cached = pl.ds(pl.multiple_of(t0 * seq, span), span)
-                out = jnp.dot(pb[slot, n].astype(BF), vals[cached, :], preferred_element_type=F32)
-                v_new = qkv[pl.ds(t0, 8), (groups + 1) * head:].astype(BF).astype(F32)
-                outs.append([out[8 * j:8 * (j + 1)] + pob[slot, n, 8 * j:8 * (j + 1), :] * v_new for j in range(groups)])
+                t0, rows, cached = block(g, n)
+                p = pb[slot, n].astype(BF)
+                v_new = jnp.concatenate([qkv[rows, (groups + 1) * head:].astype(BF), none], axis=0)
+                outs.append(jnp.dot(p[:, 0:span], vals[cached, :], preferred_element_type=F32)
+                            + jnp.dot(p[:, span:], v_new, preferred_element_type=F32))
+            rows = pl.ds(pl.multiple_of(block(g, n0)[0], 16), 16)
             for j in range(groups):
-                both = jnp.concatenate([outs[0][j], outs[1][j]], axis=0).astype(BF)
-                h_ref[pl.ds(pl.multiple_of(start_of(g, n0), 16), 16), head * j:head * (j + 1)] = both
-
-    @pl.loop(0, n_groups + 3)
+                both = jnp.concatenate([o[8 * j:8 * (j + 1)] for o in outs], axis=0).astype(BF)
+                h_ref[rows, head * j:head * (j + 1)] = both
+
+    @pl.loop(0, n_groups + 2)
     def _(i):
-        for lag, stage in ((3, mix), (2, weigh), (1, score), (0, project)):
+        for lag, stage in ((2, mix), (1, weigh), (0, score)):
             stage(jnp.clip(i - lag, 0, n_groups - 1))
 
 
@@ -131,8 +147,8 @@
     pl.semaphore_wait(barrier, len(peers))
 
 
-def front_kernel(layer, dims, gathered, x_hbm, bound, cos, sin, gain, wq, wk, wv, wg, wu, kc, vc, h_ref,
-                 x, a, inv_ref, qkv_w, gate_w, up_w, qkv, gate, up, keys, vals, qb, ob, lb, pb, pob, x_sem, w_sem, kv_sem,
+def front_kernel(layer, dims, gathered, x_hbm, lens, table, gain, wq, wk, wv, wg, wu, kc, vc, h_ref,
+                 x, a, inv_ref, qkv_w, gate_w, up_w, qkv, gate, up, keys, vals, lb, pb, x_sem, w_sem, kv_sem,
                  sums=None, sum_s=None, sum_r=None, ag_s=None, ag_r=None):
     groups, head, seq, kb, steps = dims
     qw = groups * head
@@ -187,7 +203,7 @@
             by_row = jnp.broadcast_to(jnp.sum(total, axis=-1, keepdims=True), (128, 128))
             sums[me, :, c0:c0 + 128] = by_row.T[0:8]
         swap_sums = [remote(sums.at[me], sums.at[me], sum_s.at[n], sum_r.at[n], peer) for n, peer in enumerate(peers)]
-        for copy in swap_sums + near + to_mate[:1]:
+        for copy in swap_sums + near[:1] + to_mate[:1]:
             copy.start()
         for n, copy in enumerate(swap_sums):
             sender = lax.rem(me + 7 - n, 8)
@@ -201,8 +217,12 @@
     else:
         x_copy = pltpu.make_async_copy(x_hbm, x, x_sem)
         x_copy.start()
-        start_weights(0, 0)
+        early = weights(0, 0)
+        for copy in early[0]:
+            copy.start()
         x_copy.wait()
+        for copy in early[1] + early[2]:
+            copy.start()
 
         @pl.loop(0, rows // 128)
         def _(i):
@@ -237,7 +257,7 @@
             for part, device in enumerate(devices):
                 for c0 in range(0, cw, 128):
                     cs = pl.ds(pl.multiple_of(device * cw + c0, 128), 128)
-                    a[r, part * cw + c0:part * cw + c0 + 128] = (x[r, cs].astype(F32) * inv * gain[layer:layer + 1, cs]).astype(BF)
+                    a[r, part * cw + c0:part * cw + c0 + 128] = (x[r, cs].astype(F32) * inv * gain[layer:layer + 1, cs].astype(F32)).astype(BF)
 
         first = step == 0
         w_copies = weights(step, slot)
@@ -262,6 +282,8 @@
         if gathered:
             @pl.when(step == 0)
             def _():
+                near[0].wait_send()
+                near[1].start()
                 near[0].wait_recv()
                 to_mate[1].start()
                 far[0].start()
@@ -284,7 +306,7 @@
                 to_mate[4].start()
 
     if gathered:
-        for copy in swap_sums + near + far + to_mate:
+        for copy in swap_sums + near[1:] + far + to_mate:
             copy.wait_send()
 
     @pl.loop(0, rows // 32)
@@ -294,9 +316,10 @@
         u_in = up[r, :].astype(BF).astype(F32)
         h_ref[r, qw:qw + ff] = (g_in * (1.0 / (1.0 + jnp.exp(-g_in))) * u_in).astype(BF)
 
+    rotate(qkv, lens, table, groups, head)
     for copy in kv:
         copy.wait()
-    attention(qkv, cos, sin, bound, keys, vals, h_ref, (qb, ob, lb, pb, pob), groups, head, seq)
+    attention(qkv, lens, keys, vals, h_ref, (lb, pb), groups, head, seq)
 
 
 def front_call(layer, dims, rows, width, qw, ff, name, gathered=False):
@@ -308,16 +331,14 @@
     return pl.pallas_call(
         functools.partial(front_kernel, layer, dims, gathered),
         out_shape=jax.ShapeDtypeStruct((rows, qw + ff), BF),
-        in_specs=[hbm, vmem, vmem, vmem, vmem] + [hbm] * 7,
+        in_specs=[hbm, vmem, vmem, vmem] + [hbm] * 7,
         out_specs=vmem,
         scratch_shapes=[
             pltpu.VMEM((rows, width), BF), pltpu.VMEM((rows, kb), BF), pltpu.VMEM((rows, 128), F32),
             pltpu.VMEM((2, kb, qw + 2 * head), BF), pltpu.VMEM((2, ff, kb), BF), pltpu.VMEM((2, ff, kb), BF),
             pltpu.VMEM((rows, qw + 2 * head), F32), pltpu.VMEM((rows, ff), F32), pltpu.VMEM((rows, ff), F32),
             pltpu.VMEM((rows * seq, head), BF), pltpu.VMEM((rows * seq, head), BF),
-            pltpu.VMEM((2, PER, lanes, head), F32), pltpu.VMEM((2, PER, lanes, 128), F32),
-            pltpu.VMEM((2, PER, lanes, 8 * seq), F32), pltpu.VMEM((2, PER, lanes, 8 * seq), F32),
-            pltpu.VMEM((2, PER, lanes, 128), F32),
+            pltpu.VMEM((2, PER, lanes, 8 * seq + 128), F32), pltpu.VMEM((2, PER, lanes, 8 * seq + 128), F32),
             dma, dma((2, 10)), dma((2,)),
         ] + ([pltpu.VMEM((8, 8, rows), F32), dma((7,)), dma((7,)), dma((9,)), dma((9,))] if gathered else []),
         compiler_params=pltpu.CompilerParams(vmem_limit_bytes=63 * 2**20, **({"collective_id": 2, "has_side_effects": True} if gathered else {})),
@@ -408,8 +429,10 @@
 
     if last:
         near, far, to_mate = gather_plan(me, xg, cw, ag_s, ag_r)
-        for copy in near + to_mate[:1]:
+        for copy in near[:1] + to_mate[:1]:
             copy.start()
+        near[0].wait_send()
+        near[1].start()
         for n in range(2):
             near[n].wait_recv()
             far[n].start()
@@ -421,7 +444,7 @@
             copy.wait_recv()
         out = pltpu.make_async_copy(xg, out_ref, out_sem)
         out.start()
-        for copy in near + far + to_mate:
+        for copy in near[1:] + far + to_mate:
             copy.wait_send()
         out.wait()
     for copy in pair + ici:
@@ -459,13 +482,8 @@
         groups = qw // head
         cw = width // tp
         kb = 2 * cw
-        inv_freq = 1.0 / (ROPE_BASE ** (jnp.arange(0, head, 2).astype(F32) / head))
-        angles = lengths.astype(F32)[:, None] * inv_freq[None, :]
-        cos, sin = jnp.cos(angles), jnp.sin(angles)
-        cos = jnp.concatenate([cos, cos], axis=1)
-        sin = jnp.concatenate([-sin, sin], axis=1)
-        bound = jnp.broadcast_to(lengths[:, None], (rows, 128))
-        gain = norm_gain.astype(F32)
+        lens = jnp.broadcast_to(lengths.astype(F32)[:, None], (rows, 128))
+        table = jnp.asarray(angle_table(seq, head))
         gate_t, up_t = jnp.swapaxes(w_gate, 1, 2), jnp.swapaxes(w_up, 1, 2)
         kc = k_cache.reshape(layers, rows * seq, head)
         vc = v_cache.reshape(layers, rows * seq, head)
@@ -474,7 +492,7 @@
             last = layer == layers - 1
             dims = (groups, head, seq, kb, width // kb)
             h = front_call(layer, dims, rows, width, qw, ff, f"front{layer}", layer > 0)(
-                x, bound, cos, sin, gain, w_q, w_k, w_v, gate_t, up_t, kc, vc)
+                x, lens, table, norm_gain, w_q, w_k, w_v, gate_t, up_t, kc, vc)
             x = back_call(layer, f"back{layer}", layer, last, rows, width, cw, qw, ff)(h, x, w_o, w_down)
         return x
 

time: 245 us -> 224 us (0.914)
  Pallas kernels: 233 us -> 217 us
  other arithmetic: 4.04 us -> 0.68 us
    pallas_call x2, Pallas kernels: 120 us -> 103 us  [per_device(): front_call(layer, dims, rows, width, qw, ff, f'front{layer}', layer > 0)]
where the time goes in v3:
time: 224 us; the launch traced here: 223 us
  Pallas kernels  217 us (97%)
  local copies, waits for them, and re-layouts  6.01 us (3%)
    pallas_call x2, Pallas kernels, per_device(): back_call(layer, f'back{layer}', layer, last, rows, width, cw, qw, ff)  114 us
    pallas_call x2, Pallas kernels, per_device(): front_call(layer, dims, rows, width, qw, ff, f'front{layer}', layer > 0)  103 us
    unnamed x1, local copies, waits for them, and re-layouts  5.18 us

profile of v3, /device:TPU:0, one launch (start us, length us, event | category | flops | bytes accessed | tf_op | source)
XLA Modules:
  0.0 223.5 jit_solution(15725439037953131956)
XLA Ops:
  0.0 0.7 convert_element_type.3
  0.7 0.8 broadcast_in_dim.2.lens
  1.5 46.8 %front0.1.h_hbm = bf16[512,2368]{1,0:T(8,128)(2,1)} custom-call(bf16[512,5120]{1,0:T(8,128)(2,1)} %x_hbm.3, f32[512,128]{1,0:T(8,128)} %broadcast_in_dim.2.lens, f32[128,256]{1,0:T(8,128)} %constant.2.clone.table, bf16[2,5120]{1,0:T(2,128)(2,1)} %gain.3, bf16[2,5120,640]{2,1,0:T(8,128)(2,1)} %wq.3, bf16[2,5120,128]{2,1,0:T(8,128)(2,1)} %wk.3, ...), custom_call_target="tpu_custom_call" | custom-call | tf_op jit(solution)/shard_map/front0/pallas_call | solution.py:494
  48.3 44.6 %back0.1.x_hbm = bf16[512,640]{1,0:T(8,128)(2,1)} custom-call(bf16[512,2368]{1,0:T(8,128)(2,1)} %front0.1.h_hbm, bf16[512,5120]{1,0:T(8,128)(2,1)} %x_hbm.3, bf16[2,640,5120]{2,1,0:T(8,128)(2,1)} %wo.3, bf16[2,1728,5120]{2,1,0:T(8,128)(2,1)} %wd.3), custom_call_target="tpu_custom_call" | custom-call | tf_op jit(solution)/shard_map/back0/pallas_call | solution.py:496
  93.0 56.3 %front1.1.h_hbm = bf16[512,2368]{1,0:T(8,128)(2,1)} custom-call(bf16[512,640]{1,0:T(8,128)(2,1)} %back0.1.x_hbm, f32[512,128]{1,0:T(8,128)} %broadcast_in_dim.2.lens, f32[128,256]{1,0:T(8,128)} %constant.2.clone.table, bf16[2,5120]{1,0:T(2,128)(2,1)} %gain.3, bf16[2,5120,640]{2,1,0:T(8,128)(2,1)} %wq.3, bf16[2,5120,128]{2,1,0:T(8,128)(2,1)} %wk.3, ...), custom_call_target="tpu_custom_call" | custom-call | tf_op jit(solution)/shard_map/front1/pallas_call | solution.py:494
  149.2 69.1 %back1.1 = bf16[512,5120]{1,0:T(8,128)(2,1)} custom-call(bf16[512,2368]{1,0:T(8,128)(2,1)} %front1.1.h_hbm, bf16[512,640]{1,0:T(8,128)(2,1)} %back0.1.x_hbm, bf16[2,640,5120]{2,1,0:T(8,128)(2,1)} %wo.3, bf16[2,1728,5120]{2,1,0:T(8,128)(2,1)} %wd.3), custom_call_target="tpu_custom_call" | custom-call | tf_op jit(solution)/shard_map/back1/pallas_call | solution.py:496
  218.3 5.2 %copy.15 = bf16[512,5120]{1,0:T(8,128)(2,1)} copy(bf16[512,5120]{1,0:T(8,128)(2,1)} %back1.1) | data formatting | bytes 10485760

commit v4 on v0

v4 whole, which is shorter than its diff:
```python
import functools
import types

import jax
import jax.numpy as jnp
import numpy as np
from jax import lax
from jax.experimental import pallas as pl
from jax.experimental.pallas import tpu as pltpu
from jax.sharding import PartitionSpec as P

NORM_EPS = 1e-5
ROPE_BASE = 500000.0
MESH = pl.DeviceIdType.MESH
BF, F32 = jnp.bfloat16, jnp.float32
PER = 4
NT_DIMS = (((1,), (1,)), ((), ()))


def angle_table(seq, head):
    freq = np.float32(1.0) / np.power(np.float32(ROPE_BASE), np.arange(0, head, 2, dtype=np.float32) / np.float32(head))
    angle = np.arange(seq, dtype=np.float32)[:, None] * freq[None, :]
    cos, sin = np.cos(angle.astype(np.float64)), np.sin(angle.astype(np.float64))
    table = np.zeros((128, 2 * head), np.float32)
    table[:seq] = np.concatenate([cos, cos, -sin, sin], axis=1)
    return table


def rotate(qkv, lens, table, groups, head):
    at = lax.broadcasted_iota(jnp.int32, (head, head), 0)
    to = lax.broadcasted_iota(jnp.int32, (head, head), 1)
    swap = (at == lax.rem(to + head // 2, head)).astype(BF)

    @pl.loop(0, qkv.shape[0] // 128)
    def _(i):
        r = pl.ds(pl.multiple_of(i * 128, 128), 128)
        spot = lax.broadcasted_iota(jnp.int32, (128, 128), 1).astype(F32)
        hot = (lens[r, :] == spot).astype(F32)
        angle = jnp.dot(hot, table[...], precision=lax.Precision.HIGHEST, preferred_element_type=F32)
        c, s = angle[:, 0:head], angle[:, head:2 * head]
        for j in range(groups + 1):
            v = qkv[r, head * j:head * (j + 1)].astype(BF)
            other = jnp.dot(v, swap, preferred_element_type=F32)
            qkv[r, head * j:head * (j + 1)] = v.astype(F32) * c + other * s


def attention(qkv, lens, keys, vals, h_ref, bufs, groups, head, seq):
    lb, pb = bufs
    per = lb.shape[1]
    span = 8 * seq
    n_groups = qkv.shape[0] // (8 * per)
    scale = head ** -0.5
    col = lax.broadcasted_iota(jnp.int32, (8, span), 1).astype(F32)
    low = (lax.broadcasted_iota(jnp.int32, (8, span), 0) * seq).astype(F32)
    own = lax.broadcasted_iota(jnp.int32, (8, 128), 0) == lax.broadcasted_iota(jnp.int32, (8, 128), 1)
    none = jnp.zeros((120, head), BF)

    def block(g, n):
        t0 = pl.multiple_of(g * (8 * per) + 8 * n, 8)
        return t0, pl.ds(t0, 8), pl.ds(pl.multiple_of(t0 * seq, span), span)

    def score(g):
        slot = lax.rem(g, 2)
        for n in range(per):
            t0, rows, cached = block(g, n)
            q = jnp.concatenate([qkv[rows, head * j:head * (j + 1)] for j in range(groups)], axis=0).astype(BF)
            k_new = jnp.concatenate([qkv[rows, groups * head:(groups + 1) * head].astype(BF), none], axis=0)
            old = lax.dot_general(q, keys[cached, :], NT_DIMS, preferred_element_type=F32) * scale
            new = lax.dot_general(q, k_new, NT_DIMS, preferred_element_type=F32) * scale
            high = jnp.concatenate([lens[rows, :]] * (span // 128), axis=1) + low
            keep = (col >= low) & (col < high)
            for j in range(groups):
                r = slice(8 * j, 8 * (j + 1))
                lb[slot, n, r, 0:span] = jnp.where(keep, old[r], -jnp.inf)
                lb[slot, n, r, span:] = jnp.where(own, new[r], -jnp.inf)

    def weigh(g):
        slot = lax.rem(g, 2)
        for n in range(per):
            for j in range(groups):
                r = slice(8 * j, 8 * (j + 1))
                logits = [lb[slot, n, r, c0:c0 + 128] for c0 in range(0, span + 128, 128)]
                peak = jnp.max(functools.reduce(jnp.maximum, logits), axis=-1, keepdims=True)
                w = [jnp.exp(v - peak) for v in logits]
                inv = 1.0 / jnp.sum(functools.reduce(jnp.add, w), axis=-1, keepdims=True)
                for m, v in enumerate(w):
                    pb[slot, n, r, 128 * m:128 * (m + 1)] = v * inv

    def mix(g):
        slot = lax.rem(g, 2)
        for n0 in range(0, per, 2):
            outs = []
            for n in (n0, n0 + 1):
                t0, rows, cached = block(g, n)
                p = pb[slot, n].astype(BF)
                v_new = jnp.concatenate([qkv[rows, (groups + 1) * head:].astype(BF), none], axis=0)
                outs.append(jnp.dot(p[:, 0:span], vals[cached, :], preferred_element_type=F32)
                            + jnp.dot(p[:, span:], v_new, preferred_element_type=F32))
            rows = pl.ds(pl.multiple_of(block(g, n0)[0], 16), 16)
            for j in range(groups):
                both = jnp.concatenate([o[8 * j:8 * (j + 1)] for o in outs], axis=0).astype(BF)
                h_ref[rows, head * j:head * (j + 1)] = both

    @pl.loop(0, n_groups + 2)
    def _(i):
        for lag, stage in ((2, mix), (1, weigh), (0, score)):
            stage(jnp.clip(i - lag, 0, n_groups - 1))


def place(core, chip, fx, fy):
    x, y = lax.rem(chip, 2), chip // 2
    return 2 * (y + fy * (1 - 2 * y)) + (x + fx * (1 - 2 * x))


def remote(src, dst, send_sem, recv_sem, device):
    return pltpu.make_async_remote_copy(src_ref=src, dst_ref=dst, send_sem=send_sem, recv_sem=recv_sem,
                                        device_id={"tp": device}, device_id_type=MESH)


def columns(device, width):
    return pl.ds(pl.multiple_of(device * width, width), width)


def gather_plan(me, xg, cw, send_sem, recv_sem):
    core, chip = lax.rem(me, 2), me // 2
    mate = me + 1 - 2 * core
    first = 2 * place(core, chip, 1 - core, core) + core
    second = 2 * place(core, chip, core, 1 - core) + core
    across = 2 * (3 - chip) + core
    rows = xg.shape[0]
    half = rows // 2

    def share(n, r0, r1, owner, device):
        block = xg.at[r0:r1, columns(owner, cw)]
        return remote(block, block, send_sem.at[n], recv_sem.at[n], device)

    near = [share(0, 0, rows, me, first), share(1, 0, rows, me, second)]
    far = [share(2, 0, half, first, second), share(3, half, rows, second, first)]
    to_mate = [share(4, 0, rows, me, mate), share(5, 0, rows, first, mate), share(6, 0, rows, second, mate),
               share(7, 0, half, across, mate), share(8, half, rows, across, mate)]
    return near, far, to_mate


def greet(me, peers):
    barrier = pltpu.get_barrier_semaphore()
    for device in peers:
        pl.semaphore_signal(barrier, inc=1, device_id={"tp": device}, device_id_type=MESH)
    pl.semaphore_wait(barrier, len(peers))


UNITS = ((0, 0, 256), (0, 256, 640), (1, 0, 640), (2, 0, 640), (3, 0, 640))
SCRATCH = ("x", "a", "inv", "qkv_w", "gate_w", "up_w", "wo_w", "qkv", "gate", "up", "keys", "vals", "lb", "pb", "h", "recv_p",
           "recv_i", "sums", "x_sem", "w_sem", "kv_sem", "out_w_sem", "pair_s", "pair_r", "ici_s", "ici_r", "sum_s", "sum_r",
           "ag_s", "ag_r", "out_sem")


def block_kernel(dims, x_hbm, lens, table, gain, wq, wk, wv, wg, wu, wo, wd, kc, vc, out_ref, *scratch):
    layers, groups, head, seq, cw, steps = dims
    m = types.SimpleNamespace(**dict(zip(SCRATCH, scratch, strict=True)))
    x, h = m.x, m.h
    rows, width = x.shape
    qw, ff, kb = groups * head, m.gate.shape[1], 2 * cw
    n_units, n_peers = len(UNITS), width // cw
    me = lax.axis_index("tp")
    core, chip = lax.rem(me, 2), me // 2
    mate = me + 1 - 2 * core
    order = (place(core, chip, 1, 1), place(core, chip, 0, 1), place(core, chip, 1, 0), chip)
    peers = [lax.rem(me + n, n_peers) for n in range(1, n_peers)]
    chunks = cw // 128

    def start(copies):
        for copy in copies:
            copy.start()

    def sources(step):
        moved, both = (step + 2) // 3, step // 3
        swap = step // 2 * (1 - lax.rem(step, 2))
        return 2 * place(core, chip, moved, both) + swap, 2 * place(core, chip, both, moved) + 1 - swap

    def in_weights(layer, step, slot):
        found = ([], [], [])
        for part, device in enumerate(sources(step)):
            ks, to = columns(device, cw), slice(part * cw, (part + 1) * cw)
            pairs = (
                (0, wq.at[layer, ks, :], m.qkv_w.at[slot, to, 0:qw]),
                (0, wk.at[layer, ks, :], m.qkv_w.at[slot, to, qw:qw + head]),
                (0, wv.at[layer, ks, :], m.qkv_w.at[slot, to, qw + head:qw + 2 * head]),
                (1, wg.at[layer, :, ks], m.gate_w.at[slot, :, to]),
                (2, wu.at[layer, :, ks], m.up_w.at[slot, :, to]),
            )
            for n, (which, src, dst) in enumerate(pairs):
                found[which].append(pltpu.make_async_copy(src, dst, m.w_sem.at[slot, part * 5 + n]))
        return found

    def down_w(i):
        return (m.gate_w, m.up_w)[i % 2].at[i // 2]

    def out_weights(layer, u, which):
        i, c0, c1 = UNITS[u]
        copies = []
        for n, device in enumerate((2 * order[i] + 1 - core, 2 * order[i] + core)):
            at = 2 * c0 + n * (c1 - c0)
            src, dst = ((wd, down_w(i)), (wo, m.wo_w.at[i % 2]))[which]
            copies.append(pltpu.make_async_copy(
                src.at[layer, :, pl.ds(pl.multiple_of(device * cw + c0, 128), c1 - c0)],
                dst.at[:, at:at + c1 - c0], m.out_w_sem.at[u, 2 * which + n]))
        return copies

    def start_out_weights(layer, tiles, whiches):
        for u, (i, _, _) in enumerate(UNITS):
            if i in tiles:
                for which in whiches:
                    start(out_weights(layer, u, which))

    def front(layer, gather):
        kv = [pltpu.make_async_copy(kc.at[layer], m.keys, m.kv_sem.at[0]),
              pltpu.make_async_copy(vc.at[layer], m.vals, m.kv_sem.at[1])]
        if gather:
            near, far, to_mate = gather

        @pl.loop(0, steps)
        def _(step):
            slot = lax.rem(step, 2)
            if gather:
                for n in range(3):
                    @pl.when(step == n)
                    def _(n=n):
                        to_mate[n].wait_recv()

                @pl.when(step == 3)
                def _():
                    to_mate[3].wait_recv()
                    to_mate[4].wait_recv()

            devices = sources(step)

            @pl.loop(0, rows // 64)
            def _(i):
                r = pl.ds(pl.multiple_of(i * 64, 64), 64)
                inv = m.inv[r, :]
                for part, device in enumerate(devices):
                    for c0 in range(0, cw, 128):
                        cs = pl.ds(pl.multiple_of(device * cw + c0, 128), 128)
                        g = gain[layer:layer + 1, cs].astype(F32)
                        m.a[r, part * cw + c0:part * cw + c0 + 128] = (x[r, cs].astype(F32) * inv * g).astype(BF)

            first = step == 0
            w_copies = in_weights(layer, step, slot)
            for copy in w_copies[0]:
                copy.wait()
            part = jnp.dot(m.a[...], m.qkv_w[slot], preferred_element_type=F32)
            m.qkv[...] = jnp.where(first, 0.0, m.qkv[...]) + part
            for copy in w_copies[1]:
                copy.wait()
            if not gather:
                @pl.when(first)
                def _():
                    for copies in in_weights(layer, 1, 1):
                        start(copies)

            part = lax.dot_general(m.a[...], m.gate_w[slot], NT_DIMS, preferred_element_type=F32)
            m.gate[...] = jnp.where(first, 0.0, m.gate[...]) + part
            if gather:
                @pl.when(step == 0)
                def _():
                    near[0].wait_send()
                    near[1].start()
                    near[0].wait_recv()
                    to_mate[1].start()
                    far[0].start()
            for copy in w_copies[2]:
                copy.wait()
            part = lax.dot_general(m.a[...], m.up_w[slot], NT_DIMS, preferred_element_type=F32)
            m.up[...] = jnp.where(first, 0.0, m.up[...]) + part
            if gather:
                @pl.when(step == 1)
                def _():
                    near[1].wait_recv()
                    to_mate[2].start()
                    far[1].start()

                @pl.when(step == 2)
                def _():
                    far[0].wait_recv()
                    to_mate[3].start()
                    far[1].wait_recv()
                    to_mate[4].start()

            @pl.when(step + 2 < steps)
            def _():
                for copies in in_weights(layer, step + 2, slot):
                    start(copies)

            @pl.when(step == 1)
            def _():
                start(kv)

            @pl.when(step == 2)
            def _():
                start_out_weights(layer, (0, 1), (0, 1))

        if gather:
            for copy in near[1:] + far + to_mate:
                copy.wait_send()
        start_out_weights(layer, (2, 3), (0,))

        @pl.loop(0, rows // 32)
        def _(i):
            r = pl.ds(pl.multiple_of(i * 32, 32), 32)
            g_in = m.gate[r, :].astype(BF).astype(F32)
            u_in = m.up[r, :].astype(BF).astype(F32)
            h[r, qw:qw + ff] = (g_in * (1.0 / (1.0 + jnp.exp(-g_in))) * u_in).astype(BF)

        rotate(m.qkv, lens, table, groups, head)
        for copy in kv:
            copy.wait()
        attention(m.qkv, lens, m.keys, m.vals, h, (m.lb, m.pb), groups, head, seq)

    def back(layer):
        last = layer == layers - 1
        pair, ici = [], []
        for u, (i, c0, c1) in enumerate(UNITS):
            held = slice(i % 2 * cw + c0, i % 2 * cw + c1)
            pair.append(remote(m.gate.at[:, held], m.recv_p.at[i, :, c0:c1], m.pair_s.at[layer, u], m.pair_r.at[layer, u], mate))
            if i < 3:
                block = pl.ds((i * chunks + c0 // 128) * rows, (c1 - c0) // 128 * rows)
                ici.append(remote(m.keys.at[block], m.recv_i.at[block], m.ici_s.at[layer, u], m.ici_r.at[layer, u],
                                  2 * order[i] + core))

        def settle(u):
            i, c0, c1 = UNITS[u]
            pair[u].wait_recv()
            if i < 3:
                @pl.loop(0, rows // 64)
                def _(n):
                    r = pl.ds(pl.multiple_of(n * 64, 64), 64)
                    for c in range(c0, c1, 128):
                        both = m.up[r, i % 2 * cw + c:i % 2 * cw + c + 128] + m.recv_p[i, r, c:c + 128]
                        to = pl.ds(pl.multiple_of((i * chunks + c // 128) * rows + n * 64, 64), 64)
                        m.keys[to, :] = both.astype(BF)
                ici[u].start()

        for u, (i, c0, c1) in enumerate(UNITS):
            held = i % 2 * cw
            if i >= 2:
                for v in range(n_units):
                    if UNITS[v][0] == i - 2:
                        pair[v].wait_send()
            for which in range(2):
                for copy in out_weights(layer, u, which):
                    copy.wait()
            part = (jnp.dot(h[:, 0:qw], m.wo_w[i % 2, :, 2 * c0:2 * c1], preferred_element_type=F32)
                    + jnp.dot(h[:, qw:qw + ff], down_w(i)[:, 2 * c0:2 * c1], preferred_element_type=F32))
            m.gate[:, held + c0:held + c1] = part[:, 0:c1 - c0]
            pair[u].start()
            m.up[:, held + c0:held + c1] = part[:, c1 - c0:]
            if u == n_units - 1 or UNITS[u + 1][0] != i:
                if i < 2:
                    start_out_weights(layer, (i + 2,), (1,))
                if i % 2 and not last:
                    for copies in in_weights(layer + 1, i // 2, i // 2):
                        start(copies)
            if u >= 1:
                settle(u - 1)
        settle(n_units - 1)
        for copy in ici:
            copy.wait_recv()

        @pl.loop(0, rows // 128)
        def _(n):
            r = pl.ds(pl.multiple_of(n * 128, 128), 128)
            squares = jnp.zeros((128, 128), F32)
            for c in range(chunks):
                cs = pl.ds(pl.multiple_of(me * cw + c * 128, 128), 128)
                total = m.up[r, cw + c * 128:cw + (c + 1) * 128] + m.recv_p[3, r, c * 128:(c + 1) * 128]
                for i in range(3):
                    at = pl.ds(pl.multiple_of((i * chunks + c) * rows + n * 128, 128), 128)
                    total = total + m.recv_i[at, :].astype(F32)
                new = (x[r, cs].astype(F32) + total).astype(BF)
                x[r, cs] = new
                squares = squares + new.astype(F32) * new.astype(F32)
            if not last:
                by_row = jnp.broadcast_to(jnp.sum(squares, axis=-1, keepdims=True), (128, 128))
                m.sums[me, :, r] = by_row.T[0:8]

        gather = gather_plan(me, x, cw, m.ag_s.at[layer], m.ag_r.at[layer])
        near, far, to_mate = gather
        swap_sums = [] if last else [remote(m.sums.at[me], m.sums.at[me], m.sum_s.at[n], m.sum_r.at[n], peer)
                                     for n, peer in enumerate(peers)]
        start(swap_sums + near[:1] + to_mate[:1])
        for copy in ici:
            copy.wait_send()
        for u, (i, _, _) in enumerate(UNITS):
            if i >= 2:
                pair[u].wait_send()
        if not last:
            for n in range(n_peers - 1):
                sender = lax.rem(me + n_peers - 1 - n, n_peers)
                remote(m.sums.at[sender], m.sums.at[sender], m.sum_s.at[n], m.sum_r.at[n], sender).wait_recv()
            for c0 in range(0, rows, 128):
                total = m.sums[0, :, c0:c0 + 128]
                for n in range(1, n_peers):
                    total = total + m.sums[n, :, c0:c0 + 128]
                scale = lax.rsqrt(total / width + NORM_EPS)
                m.inv[c0:c0 + 128, :] = jnp.broadcast_to(scale[0:1], (128, 128)).T
            for copy in swap_sums:
                copy.wait_send()
        return gather

    x_copy = pltpu.make_async_copy(x_hbm, x, m.x_sem)
    x_copy.start()
    early = in_weights(0, 0, 0)
    start(early[0])
    greet(me, peers)
    x_copy.wait()
    start(early[1] + early[2])

    @pl.loop(0, rows // 128)
    def _(i):
        r = pl.ds(pl.multiple_of(i * 128, 128), 128)
        total = jnp.zeros((128, 128), F32)
        for c0 in range(0, width, 128):
            v = x[r, c0:c0 + 128].astype(F32)
            total = total + v * v
        mean = jnp.sum(total, axis=-1, keepdims=True) / width
        m.inv[r, :] = jnp.broadcast_to(lax.rsqrt(mean + NORM_EPS), (128, 128))

    gather = None
    for layer in range(layers):
        front(layer, gather)
        gather = back(layer)

    near, far, to_mate = gather

    def store(n, q):
        block = pl.ds(pl.multiple_of(q * kb, kb), kb)
        return pltpu.make_async_copy(x.at[:, block], out_ref.at[:, block], m.out_sem.at[n])

    out = [store(n, q) for n, q in enumerate((chip, order[2], order[1], order[0]))]
    near[0].wait_send()
    near[1].start()
    for n in range(2):
        near[n].wait_recv()
        far[n].start()
        to_mate[1 + n].start()
    to_mate[0].wait_recv()
    out[0].start()
    for n in range(2):
        far[n].wait_recv()
        to_mate[3 + n].start()
    to_mate[1].wait_recv()
    to_mate[2].wait_recv()
    out[1].start()
    out[2].start()
    to_mate[3].wait_recv()
    to_mate[4].wait_recv()
    out[3].start()
    for copy in near[1:] + far + to_mate:
        copy.wait_send()
    for copy in out:
        copy.wait()


def block_call(layers, rows, width, cw, groups, head, seq, ff):
    hbm = pl.BlockSpec(memory_space=pl.ANY)
    vmem = pl.BlockSpec(memory_space=pltpu.VMEM)
    dma, ram = pltpu.SemaphoreType.DMA, pltpu.VMEM
    qw, kb, n, peers = groups * head, 2 * cw, len(UNITS), width // cw
    joint = (2, PER, groups * 8, 8 * seq + 128)
    return pl.pallas_call(
        functools.partial(block_kernel, (layers, groups, head, seq, cw, width // kb)),
        out_shape=jax.ShapeDtypeStruct((rows, width), BF),
        in_specs=[hbm, vmem, vmem, vmem] + [hbm] * 9,
        out_specs=hbm,
        scratch_shapes=[
            ram((rows, width), BF), ram((rows, kb), BF), ram((rows, 128), F32),
            ram((2, kb, qw + 2 * head), BF), ram((2, ff, kb), BF), ram((2, ff, kb), BF), ram((2, qw, kb), BF),
            ram((rows, qw + 2 * head), F32), ram((rows, ff), F32), ram((rows, ff), F32),
            ram((rows * seq, head), BF), ram((rows * seq, head), BF), ram(joint, F32), ram(joint, F32),
            ram((rows, qw + ff), BF), ram((4, rows, cw), F32), ram((3 * cw // 128 * rows, 128), BF), ram((peers, 8, rows), F32),
            dma, dma((2, 10)), dma((2,)), dma((n, 4)), dma((layers, n)), dma((layers, n)), dma((layers, n)), dma((layers, n)),
            dma((peers - 1,)), dma((peers - 1,)), dma((layers, 9)), dma((layers, 9)), dma((4,)),
        ],
        compiler_params=pltpu.CompilerParams(vmem_limit_bytes=67043328, collective_id=0, has_side_effects=True),
        name="mega",
    )


def solution(mesh):
    tp = mesh.shape["tp"]
    arg_specs = (P("dp", None), P("dp"), P(), P(None, None, "tp"), P(None, None, "tp"), P(None, None, "tp"), P(None, "tp", None), P(None, None, "tp"), P(None, None, "tp"), P(None, "tp", None), P(None, "dp", None, "tp", None), P(None, "dp", None, "tp", None))

    def per_device(x_in, lengths, norm_gain, w_q, w_k, w_v, w_o, w_gate, w_up, w_down, k_cache, v_cache):
        rows, width = x_in.shape
        layers, _, seq, _, head = k_cache.shape
        qw, ff = w_q.shape[-1], w_gate.shape[-1]
        groups = qw // head
        cw = width // tp
        lens = jnp.broadcast_to(lengths.astype(F32)[:, None], (rows, 128))
        table = jnp.asarray(angle_table(seq, head))
        gate_t, up_t = jnp.swapaxes(w_gate, 1, 2), jnp.swapaxes(w_up, 1, 2)
        kc = k_cache.reshape(layers, rows * seq, head)
        vc = v_cache.reshape(layers, rows * seq, head)
        return block_call(layers, rows, width, cw, groups, head, seq, ff)(
            x_in, lens, table, norm_gain, w_q, w_k, w_v, gate_t, up_t, w_o, w_down, kc, vc)

    return jax.shard_map(per_device, mesh=mesh, in_specs=arg_specs, out_specs=P("dp", None), check_vma=False)
```

time: 444 us -> 202 us (0.45); the launches traced: 437 us -> 202 us
  Pallas kernels: 0 us -> 196 us
  matrix products: 166 us -> 0 us
  waiting for transfers between devices: 133 us -> 0 us
  blocking collectives: 62.8 us -> 0 us
  other arithmetic: 32.2 us -> 0.68 us
  local copies, waits for them, and re-layouts: 22.7 us -> 6.02 us
  between operations: 14.2 us -> 0.01 us
  starting transfers between devices: 5.71 us -> 0 us
    pallas_call x0 -> x1, Pallas kernels: none -> 196 us  [per_device(): block_call(layers, rows, width, cw, groups, head, seq, ff)]
    dot_general x18 -> x0, matrix products: 166 us -> none  [the longest x2 33.3 us: layer_update(): jnp.dot(normed, wu_layer, preferred_element_type=jnp.float32)]
    all_gather x2 -> x0, waiting for transfers between devices: 72.9 us -> none  [per_device(): x_res = lax.all_gather(new_cols, 'tp', axis=1, tiled=True)]
    all_to_all x1 -> x0, blocking collectives: 62.8 us -> none  [per_device(): received = lax.all_to_all(partial_sum, 'tp', 1, 0, tiled=True)]
    all_to_all x1 -> x0, waiting for transfers between devices: 60.4 us -> none  [per_device(): received = lax.all_to_all(partial_sum, 'tp', 1, 0, tiled=True)]
    reduce_sum x6 -> x0, other arithmetic: 16.2 us -> none  [the longest x2 7.32 us: rms_norm(): jnp.mean(x_f32 * x_f32, axis=-1, keepdims=True) + NORM_EPS]
    unnamed x31 -> x1, local copies, waits for them, and re-layouts: 13.1 us -> 5.18 us
    all_to_all x1 -> x0, starting transfers between devices: 5.46 us -> none  [per_device(): received = lax.all_to_all(partial_sum, 'tp', 1, 0, tiled=True)]
  transfers between devices with their start and end apart: 3 -> 0, of which waited for: 3 -> 0; matrix products, arithmetic and copies ran while one was open for 0% -> 0% of each run, Pallas kernels for 0% -> 0%
where the time goes in v4:
time: 202 us
  Pallas kernels  196 us (97%)
  local copies, waits for them, and re-layouts  6.02 us (3%)
    pallas_call x1, Pallas kernels, per_device(): block_call(layers, rows, width, cw, groups, head, seq, ff)  196 us
    unnamed x1, local copies, waits for them, and re-layouts  5.18 us

profile of v4, /device:TPU:0, one launch (start us, length us, event | category | flops | bytes accessed | tf_op | source)
XLA Modules:
  0.0 202.3 jit_solution(17275266848152783121)
XLA Ops:
  0.0 0.7 convert_element_type.3
  0.7 0.8 broadcast_in_dim.2.lens
  1.5 195.6 %mega.1 = bf16[512,5120]{1,0:T(8,128)(2,1)} custom-call(bf16[512,5120]{1,0:T(8,128)(2,1)} %x_hbm.1, f32[512,128]{1,0:T(8,128)} %broadcast_in_dim.2.lens, f32[128,256]{1,0:T(8,128)} %constant.2.clone.table, bf16[2,5120]{1,0:T(2,128)(2,1)} %gain.1, bf16[2,5120,640]{2,1,0:T(8,128)(2,1)} %wq.1, bf16[2,5120,128]{2,1,0:T(8,128)(2,1)} %wk.1, ...), custom_call_target="tpu_custom_call" | custom-call | tf_op jit(solution)/shard_map/mega/pallas_call | solution.py:504
  197.1 5.2 %copy.15 = bf16[512,5120]{1,0:T(8,128)(2,1)} copy(bf16[512,5120]{1,0:T(8,128)(2,1)} %mega.1) | data formatting | bytes 10485760

commit v5 on v4

v5 whole, which is shorter than its diff:
```python
import functools
import types

import jax
import jax.numpy as jnp
import numpy as np
from jax import lax
from jax.experimental import pallas as pl
from jax.experimental.pallas import tpu as pltpu
from jax.sharding import PartitionSpec as P

NORM_EPS = 1e-5
ROPE_BASE = 500000.0
MESH = pl.DeviceIdType.MESH
BF, F32 = jnp.bfloat16, jnp.float32
PER = 4
LANE = 128
TOK = 8
NT_DIMS = (((1,), (1,)), ((), ()))


def aligned(at, size):
    return pl.ds(pl.multiple_of(at, size), size)


def angle_table(seq, head):
    freq = np.float32(1.0) / np.power(np.float32(ROPE_BASE), np.arange(0, head, 2, dtype=np.float32) / np.float32(head))
    angle = np.arange(seq, dtype=np.float32)[:, None] * freq[None, :]
    cos, sin = np.cos(angle.astype(np.float64)), np.sin(angle.astype(np.float64))
    table = np.zeros((LANE, 2 * head), np.float32)
    table[:seq] = np.concatenate([cos, cos, -sin, sin], axis=1)
    return table


def rotate(qkv, lens, table, groups, head, r0, r1):
    at = lax.broadcasted_iota(jnp.int32, (head, head), 0)
    to = lax.broadcasted_iota(jnp.int32, (head, head), 1)
    swap = (at == lax.rem(to + head // 2, head)).astype(BF)

    @pl.loop(r0 // LANE, r1 // LANE)
    def _(i):
        r = aligned(i * LANE, LANE)
        spot = lax.broadcasted_iota(jnp.int32, (LANE, LANE), 1).astype(F32)
        hot = (lens[r, :] == spot).astype(F32)
        angle = jnp.dot(hot, table[...], precision=lax.Precision.HIGHEST, preferred_element_type=F32)
        c, s = angle[:, 0:head], angle[:, head:2 * head]
        for j in range(groups + 1):
            v = qkv[r, head * j:head * (j + 1)].astype(BF)
            other = jnp.dot(v, swap, preferred_element_type=F32)
            qkv[r, head * j:head * (j + 1)] = v.astype(F32) * c + other * s


def attention(qkv, lens, keys, vals, h_ref, bufs, groups, head, seq, r0, r1):
    lb, pb = bufs
    per = lb.shape[0]
    span = TOK * seq
    g0, g1 = r0 // (TOK * per), r1 // (TOK * per)
    scale = head ** -0.5
    col = lax.broadcasted_iota(jnp.int32, (TOK, span), 1).astype(F32)
    low = (lax.broadcasted_iota(jnp.int32, (TOK, span), 0) * seq).astype(F32)
    own = lax.broadcasted_iota(jnp.int32, (TOK, LANE), 0) == lax.broadcasted_iota(jnp.int32, (TOK, LANE), 1)
    none = jnp.zeros((120, head), BF)

    def block(g, n):
        t0 = pl.multiple_of(g * (TOK * per) + 8 * n, 8)
        return t0, pl.ds(t0, 8), pl.ds(pl.multiple_of(t0 * seq, span), span)

    def score(g):
        for n in range(per):
            t0, rows, cached = block(g, n)
            q = jnp.concatenate([qkv[rows, head * j:head * (j + 1)] for j in range(groups)], axis=0).astype(BF)
            k_new = jnp.concatenate([qkv[rows, groups * head:(groups + 1) * head].astype(BF), none], axis=0)
            old = lax.dot_general(q, keys[cached, :], NT_DIMS, preferred_element_type=F32) * scale
            new = lax.dot_general(q, k_new, NT_DIMS, preferred_element_type=F32) * scale
            high = jnp.concatenate([lens[rows, :]] * (span // LANE), axis=1) + low
            keep = (col >= low) & (col < high)
            for j in range(groups):
                r = slice(TOK * j, TOK * (j + 1))
                lb[n, r, 0:span] = jnp.where(keep, old[r], -jnp.inf)
                lb[n, r, span:] = jnp.where(own, new[r], -jnp.inf)

    def weigh(_):
        for n in range(per):
            for j in range(groups):
                r = slice(TOK * j, TOK * (j + 1))
                logits = [lb[n, r, c0:c0 + LANE] for c0 in range(0, span + LANE, LANE)]
                peak = jnp.max(functools.reduce(jnp.maximum, logits), axis=-1, keepdims=True)
                w = [jnp.exp(v - peak) for v in logits]
                inv = 1.0 / jnp.sum(functools.reduce(jnp.add, w), axis=-1, keepdims=True)
                for m, v in enumerate(w):
                    pb[n, r, LANE * m:LANE * (m + 1)] = v * inv

    def mix(g):
        for n0 in range(0, per, 2):
            outs = []
            for n in (n0, n0 + 1):
                t0, rows, cached = block(g, n)
                p = pb[n].astype(BF)
                v_new = jnp.concatenate([qkv[rows, (groups + 1) * head:].astype(BF), none], axis=0)
                outs.append(jnp.dot(p[:, 0:span], vals[cached, :], preferred_element_type=F32)
                            + jnp.dot(p[:, span:], v_new, preferred_element_type=F32))
            rows = pl.ds(pl.multiple_of(block(g, n0)[0], 16), 16)
            for j in range(groups):
                both = jnp.concatenate([o[TOK * j:TOK * (j + 1)] for o in outs], axis=0).astype(BF)
                h_ref[rows, head * j:head * (j + 1)] = both

    @pl.loop(g0, g1 + 2)
    def _(i):
        for lag, stage in ((2, mix), (1, weigh), (0, score)):
            stage(jnp.clip(i - lag, g0, g1 - 1))


def place(core, chip, fx, fy):
    x, y = lax.rem(chip, 2), chip // 2
    return 2 * (y + fy * (1 - 2 * y)) + (x + fx * (1 - 2 * x))


def remote(src, dst, send_sem, recv_sem, device):
    return pltpu.make_async_remote_copy(src_ref=src, dst_ref=dst, send_sem=send_sem, recv_sem=recv_sem,
                                        device_id={"tp": device}, device_id_type=MESH)


def columns(device, width):
    return pl.ds(pl.multiple_of(device * width, width), width)


def gather_plan(me, xg, cw, send_sem, recv_sem):
    core, chip = lax.rem(me, 2), me // 2
    mate = me + 1 - 2 * core
    first = 2 * place(core, chip, 1 - core, core) + core
    second = 2 * place(core, chip, core, 1 - core) + core
    across = 2 * (3 - chip) + core
    rows = xg.shape[0]
    half = rows // 2

    def share(n, r0, r1, owner, device):
        block = xg.at[r0:r1, columns(owner, cw)]
        return remote(block, block, send_sem.at[n], recv_sem.at[n], device)

    near = [share(0, 0, rows, me, first), share(1, 0, rows, me, second)]
    far = [share(2, 0, half, first, second), share(3, half, rows, second, first)]
    to_mate = [share(4, 0, rows, me, mate), share(5, 0, rows, first, mate), share(6, 0, rows, second, mate),
               share(7, 0, half, across, mate), share(8, half, rows, across, mate)]
    return near, far, to_mate


def greet(me, peers):
    barrier = pltpu.get_barrier_semaphore()
    for device in peers:
        pl.semaphore_signal(barrier, inc=1, device_id={"tp": device}, device_id_type=MESH)
    pl.semaphore_wait(barrier, len(peers))


UNITS = ((0, 0, 256, 0, 0), (0, 256, 640, 0, 0), (1, 0, 640, 0, 0), (2, 0, 640, 0, 0),
         (0, 0, 640, 1, 1), (1, 0, 640, 1, 1), (2, 0, 640, 1, 1), (3, 0, 640, 0, 1))
EARLY = 4
PIECES = ((0, 0, 256), (0, 256, 640), (1, 0, 640), (2, 0, 640), (3, 0, 640))
SCRATCH = ("x", "a", "inv", "qkv_w", "twin_w", "wo_w", "qkv", "twin", "keys", "vals", "lb", "pb", "h", "recv_p",
           "recv_i", "sums", "x_sem", "w_sem", "kv_sem", "out_w_sem", "pair_s", "pair_r", "ici_s", "ici_r", "sum_s", "sum_r",
           "ag_s", "ag_r", "out_sem")


def block_kernel(dims, x_hbm, lens, table, gain, wq, wk, wv, wg, wu, wo, wd, kc, vc, out_ref, *scratch):
    layers, groups, head, seq, cw, steps = dims
    m = types.SimpleNamespace(**dict(zip(SCRATCH, scratch, strict=True)))
    m.gate_w, m.up_w, m.gate, m.up = m.twin_w.at[0], m.twin_w.at[1], m.twin.at[0], m.twin.at[1]
    x, h = m.x, m.h
    rows, width = x.shape
    qw, ff, kb = groups * head, m.twin.shape[2], 2 * cw
    n_units, n_peers = len(UNITS), width // cw
    me = lax.axis_index("tp")
    core, chip = lax.rem(me, 2), me // 2
    mate = me + 1 - 2 * core
    order = (place(core, chip, 1, 1), place(core, chip, 0, 1), place(core, chip, 1, 0), chip)
    peers = [lax.rem(me + n, n_peers) for n in range(1, n_peers)]
    chunks, half = cw // LANE, rows // 2

    def start(copies):
        for copy in copies:
            copy.start()

    def sources(step):
        moved, both = (step + 2) // 3, step // 3
        swap = step // 2 * (1 - lax.rem(step, 2))
        return 2 * place(core, chip, moved, both) + swap, 2 * place(core, chip, both, moved) + 1 - swap

    def in_weights(layer, step, slot):
        found = ([], [], [])
        for part, device in enumerate(sources(step)):
            ks, to = columns(device, cw), slice(part * cw, (part + 1) * cw)
            pairs = (
                (0, wq.at[layer, ks, :], m.qkv_w.at[slot, to, 0:qw]),
                (0, wk.at[layer, ks, :], m.qkv_w.at[slot, to, qw:qw + head]),
                (0, wv.at[layer, ks, :], m.qkv_w.at[slot, to, qw + head:qw + 2 * head]),
                (1, wg.at[layer, :, ks], m.gate_w.at[slot, :, to]),
                (2, wu.at[layer, :, ks], m.up_w.at[slot, :, to]),
            )
            for n, (which, src, dst) in enumerate(pairs):
                found[which].append(pltpu.make_async_copy(src, dst, m.w_sem.at[slot, part * 5 + n]))
        return found

    def down_w(i):
        return (m.gate_w, m.up_w)[i % 2].at[i // 2]

    def out_weights(layer, u, which):
        i, c0, c1 = PIECES[u]
        copies = []
        for n, device in enumerate((2 * order[i] + 1 - core, 2 * order[i] + core)):
            at = 2 * c0 + n * (c1 - c0)
            src, dst = ((wd, down_w(i)), (wo, m.wo_w.at[i % 3]))[which]
            copies.append(pltpu.make_async_copy(
                src.at[layer, :, pl.ds(pl.multiple_of(device * cw + c0, LANE), c1 - c0)],
                dst.at[:, at:at + c1 - c0], m.out_w_sem.at[u, 2 * which + n]))
        return copies

    def start_out_weights(layer, tiles, whiches):
        for u, (i, _, _) in enumerate(PIECES):
            if i in tiles:
                for which in whiches:
                    start(out_weights(layer, u, which))

    def cache(layer):
        return [pltpu.make_async_copy(kc.at[layer], m.keys, m.kv_sem.at[0]),
                pltpu.make_async_copy(vc.at[layer], m.vals, m.kv_sem.at[1])]

    def front(layer, gather):
        kv = cache(layer)
        if gather:
            near, far, to_mate = gather

        @pl.loop(0, steps)
        def _(step):
            slot = lax.rem(step, 2)
            if gather:
                for n in range(3):
                    @pl.when(step == n)
                    def _(n=n):
                        to_mate[n].wait_recv()

                @pl.when(step == 3)
                def _():
                    to_mate[3].wait_recv()
                    to_mate[4].wait_recv()

            devices = sources(step)

            @pl.loop(0, rows // 64)
            def _(i):
                r = aligned(i * 64, 64)
                inv = m.inv[r, :]
                for part, device in enumerate(devices):
                    for c0 in range(0, cw, LANE):
                        cs = aligned(device * cw + c0, LANE)
                        g = gain[layer:layer + 1, cs].astype(F32)
                        m.a[r, part * cw + c0:part * cw + c0 + LANE] = (x[r, cs].astype(F32) * inv * g).astype(BF)

            first = step == 0
            w_copies = in_weights(layer, step, slot)
            for copy in w_copies[0]:
                copy.wait()
            part = jnp.dot(m.a[...], m.qkv_w[slot], preferred_element_type=F32)
            m.qkv[...] = jnp.where(first, 0.0, m.qkv[...]) + part

            @pl.loop(0, 2)
            def _(which):
                for n in range(2):
                    @pl.when(which == n)
                    def _(n=n):
                        for copy in w_copies[1 + n]:
                            copy.wait()

                def at(k, n):
                    return jnp.logical_and(step == k, which == n)

                if not gather:
                    @pl.when(at(0, 0))
                    def _():
                        for copies in in_weights(layer, 1, 1):
                            start(copies)

                part = lax.dot_general(m.a[...], m.twin_w[which, slot], NT_DIMS, preferred_element_type=F32)
                m.twin[which] = jnp.where(first, 0.0, m.twin[which]) + part
                if gather:
                    @pl.when(at(0, 0))
                    def _():
                        near[0].wait_send()
                        near[1].start()
                        near[0].wait_recv()
                        to_mate[1].start()
                        far[0].start()

                    @pl.when(at(1, 1))
                    def _():
                        near[1].wait_recv()
                        to_mate[2].start()
                        far[1].start()

                    @pl.when(at(2, 1))
                    def _():
                        far[0].wait_recv()
                        to_mate[3].start()
                        far[1].wait_recv()
                        to_mate[4].start()

            @pl.when(step + 2 < steps)
            def _():
                for copies in in_weights(layer, step + 2, slot):
                    start(copies)

            @pl.when(step == 1)
            def _():
                start(kv)

            @pl.when(step == 2)
            def _():
                start_out_weights(layer, (0, 1), (0,))
                start_out_weights(layer, (0, 1, 2), (1,))

        if gather:
            for copy in near[1:] + far + to_mate:
                copy.wait_send()
        start_out_weights(layer, (2, 3), (0,))

    def gate_rows(r0, r1):
        @pl.loop(r0 // 32, r1 // 32)
        def _(i):
            r = aligned(i * 32, 32)
            g_in = m.gate[r, :].astype(BF).astype(F32)
            u_in = m.up[r, :].astype(BF).astype(F32)
            h[r, qw:qw + ff] = (g_in * (1.0 / (1.0 + jnp.exp(-g_in))) * u_in).astype(BF)

        rotate(m.qkv, lens, table, groups, head, r0, r1)

    def back(layer):
        last = layer == layers - 1
        pair, ici = [], []
        for u, (i, c0, c1, h0, h1) in enumerate(UNITS):
            held, r = slice(i % 2 * cw + c0, i % 2 * cw + c1), slice(h0 * half, (h1 + 1) * half)
            pair.append(remote(m.gate.at[r, held], m.recv_p.at[i % 3, r, c0:c1], m.pair_s.at[layer, u], m.pair_r.at[layer, u], mate))
            if i < 3:
                block = pl.ds(((2 * i + h0) * chunks + c0 // LANE) * half, (c1 - c0) // LANE * half)
                ici.append(remote(m.keys.at[block], m.recv_i.at[block], m.ici_s.at[layer, u], m.ici_r.at[layer, u],
                                  2 * order[i] + core))

        def settle(u):
            i, c0, c1, h0, _ = UNITS[u]
            pair[u].wait_recv()
            if i < 3:
                @pl.loop(0, half // 64)
                def _(n):
                    r = pl.ds(pl.multiple_of(h0 * half + n * 64, 64), 64)
                    for c in range(c0, c1, LANE):
                        both = m.up[r, i % 2 * cw + c:i % 2 * cw + c + LANE] + m.recv_p[i % 3, r, c:c + LANE]
                        to = pl.ds(pl.multiple_of(((2 * i + h0) * chunks + c // LANE) * half + n * 64, 64), 64)
                        m.keys[to, :] = both.astype(BF)
                ici[u].start()

        def attend(r0, r1):
            attention(m.qkv, lens, m.keys, m.vals, h, (m.lb, m.pb), groups, head, seq, r0, r1)

        gate_rows(0, half)
        for copy in cache(layer):
            copy.wait()
        attend(0, half)
        sent = set()
        loaded = set()
        for u, (i, c0, c1, h0, h1) in enumerate(UNITS):
            held, r = i % 2 * cw, slice(h0 * half, (h1 + 1) * half)
            if u == EARLY:
                gate_rows(half, rows)
                settle(u - 1)
                attend(half, rows)
            for v in range(u):
                if v not in sent and UNITS[v][0] % 2 == i % 2 and UNITS[v][0] != i and UNITS[v][3] <= h1 and UNITS[v][4] >= h0:
                    pair[v].wait_send()
                    sent.add(v)
            for p, (t, p0, p1) in enumerate(PIECES):
                if t == i and p0 < c1 and p1 > c0 and p not in loaded:
                    loaded.add(p)
                    for which in range(2):
                        for copy in out_weights(layer, p, which):
                            copy.wait()
            inner = [(p0, p1) for t, p0, p1 in PIECES if t == i and p0 < c1 and p1 > c0]
            for p0, p1 in inner:
                part = (jnp.dot(h[r, 0:qw], m.wo_w[i % 3, :, 2 * p0:2 * p1], preferred_element_type=F32)
                        + jnp.dot(h[r, qw:qw + ff], down_w(i)[:, 2 * p0:2 * p1], preferred_element_type=F32))
                m.gate[r, held + p0:held + p1] = part[:, 0:p1 - p0]
                m.up[r, held + p0:held + p1] = part[:, p1 - p0:]
            if u == n_units - 1:
                settle(u - 1)
            pair[u].start()
            if u == EARLY:
                start_out_weights(layer, (3,), (1,))
            if not last and u in (n_units - 3, n_units - 1):
                for copies in in_weights(layer + 1, u // (n_units - 1), u // (n_units - 1)):
                    start(copies)
            if u >= 1 and u not in (EARLY, n_units - 1):
                settle(u - 1)
        settle(n_units - 1)
        for copy in ici:
            copy.wait_recv()

        @pl.loop(0, rows // LANE)
        def _(n):
            r = aligned(n * LANE, LANE)
            squares = jnp.zeros((LANE, LANE), F32)
            for c in range(chunks):
                cs = aligned(me * cw + c * LANE, LANE)
                total = m.up[r, cw + c * LANE:cw + (c + 1) * LANE] + m.recv_p[0, r, c * LANE:(c + 1) * LANE]
                for i in range(3):
                    at = ((2 * i + n // (half // LANE)) * chunks + c) * half + lax.rem(n, half // LANE) * LANE
                    at = aligned(at, LANE)
                    total = total + m.recv_i[at, :].astype(F32)
                new = (x[r, cs].astype(F32) + total).astype(BF)
                x[r, cs] = new
                squares = squares + new.astype(F32) * new.astype(F32)
            if not last:
                by_row = jnp.broadcast_to(jnp.sum(squares, axis=-1, keepdims=True), (LANE, LANE))
                m.sums[me, :, r] = by_row.T[0:8]

        gather = gather_plan(me, x, cw, m.ag_s.at[layer], m.ag_r.at[layer])
        near, far, to_mate = gather
        swap_sums = [] if last else [remote(m.sums.at[me], m.sums.at[me], m.sum_s.at[n], m.sum_r.at[n], peer)
                                     for n, peer in enumerate(peers)]
        start(swap_sums + near[:1] + to_mate[:1])
        for copy in ici:
            copy.wait_send()
        for u in range(n_units):
            if u not in sent:
                pair[u].wait_send()
        if not last:
            for n in range(n_peers - 1):
                sender = lax.rem(me + n_peers - 1 - n, n_peers)
                remote(m.sums.at[sender], m.sums.at[sender], m.sum_s.at[n], m.sum_r.at[n], sender).wait_recv()
            for c0 in range(0, rows, LANE):
                total = m.sums[0, :, c0:c0 + LANE]
                for n in range(1, n_peers):
                    total = total + m.sums[n, :, c0:c0 + LANE]
                scale = lax.rsqrt(total / width + NORM_EPS)
                m.inv[c0:c0 + LANE, :] = jnp.broadcast_to(scale[0:1], (LANE, LANE)).T
            for copy in swap_sums:
                copy.wait_send()
        return gather

    x_copy = pltpu.make_async_copy(x_hbm, x, m.x_sem)
    x_copy.start()
    early = in_weights(0, 0, 0)
    start(early[0])
    greet(me, peers)
    x_copy.wait()
    start(early[1] + early[2])

    @pl.loop(0, rows // LANE)
    def _(i):
        r = aligned(i * LANE, LANE)
        total = jnp.zeros((LANE, LANE), F32)
        for c0 in range(0, width, LANE):
            v = x[r, c0:c0 + LANE].astype(F32)
            total = total + v * v
        mean = jnp.sum(total, axis=-1, keepdims=True) / width
        m.inv[r, :] = jnp.broadcast_to(lax.rsqrt(mean + NORM_EPS), (LANE, LANE))

    gather = None
    for layer in range(layers):
        front(layer, gather)
        gather = back(layer)

    near, far, to_mate = gather

    def store(n, q):
        block = pl.ds(pl.multiple_of(q * kb, kb), kb)
        return pltpu.make_async_copy(x.at[:, block], out_ref.at[:, block], m.out_sem.at[n])

    out = [store(n, q) for n, q in enumerate((chip, order[2], order[1], order[0]))]
    near[0].wait_send()
    near[1].start()
    for n in range(2):
        near[n].wait_recv()
        far[n].start()
        to_mate[1 + n].start()
    to_mate[0].wait_recv()
    out[0].start()
    for n in range(2):
        far[n].wait_recv()
        to_mate[3 + n].start()
    to_mate[1].wait_recv()
    to_mate[2].wait_recv()
    out[1].start()
    out[2].start()
    to_mate[3].wait_recv()
    to_mate[4].wait_recv()
    out[3].start()
    for copy in near[1:] + far + to_mate:
        copy.wait_send()
    for copy in out:
        copy.wait()


def block_call(layers, rows, width, cw, groups, head, seq, ff):
    hbm = pl.BlockSpec(memory_space=pl.ANY)
    vmem = pl.BlockSpec(memory_space=pltpu.VMEM)
    dma, ram = pltpu.SemaphoreType.DMA, pltpu.VMEM
    qw, kb, n, peers = groups * head, 2 * cw, len(UNITS), width // cw
    joint = (PER, groups * 8, TOK * seq + LANE)
    return pl.pallas_call(
        functools.partial(block_kernel, (layers, groups, head, seq, cw, width // kb)),
        out_shape=jax.ShapeDtypeStruct((rows, width), BF),
        in_specs=[hbm, vmem, vmem, vmem] + [hbm] * 9,
        out_specs=hbm,
        scratch_shapes=[
            ram((rows, width), BF), ram((rows, kb), BF), ram((rows, LANE), F32),
            ram((2, kb, qw + 2 * head), BF), ram((2, 2, ff, kb), BF), ram((3, qw, kb), BF),
            ram((rows, qw + 2 * head), F32), ram((2, rows, ff), F32),
            ram((rows * seq, head), BF), ram((rows * seq, head), BF), ram(joint, F32), ram(joint, F32),
            ram((rows, qw + ff), BF), ram((3, rows, cw), F32), ram((3 * cw // LANE * rows, LANE), BF), ram((peers, 8, rows), F32),
            dma, dma((2, 10)), dma((2,)), dma((len(PIECES), 4)), dma((layers, n)), dma((layers, n)), dma((layers, n)), dma((layers, n)),
            dma((peers - 1,)), dma((peers - 1,)), dma((layers, 9)), dma((layers, 9)), dma((4,)),
        ],
        compiler_params=pltpu.CompilerParams(vmem_limit_bytes=67043328, collective_id=0, has_side_effects=True),
        name="mega",
    )


def solution(mesh):
    tp = mesh.shape["tp"]
    arg_specs = (P("dp", None), P("dp"), P(), P(None, None, "tp"), P(None, None, "tp"), P(None, None, "tp"), P(None, "tp", None), P(None, None, "tp"), P(None, None, "tp"), P(None, "tp", None), P(None, "dp", None, "tp", None), P(None, "dp", None, "tp", None))

    def per_device(x_in, lengths, norm_gain, w_q, w_k, w_v, w_o, w_gate, w_up, w_down, k_cache, v_cache):
        rows, width = x_in.shape
        layers, _, seq, _, head = k_cache.shape
        qw, ff = w_q.shape[-1], w_gate.shape[-1]
        groups = qw // head
        cw = width // tp
        lens = jnp.broadcast_to(lengths.astype(F32)[:, None], (rows, LANE))
        table = jnp.asarray(angle_table(seq, head))
        gate_t, up_t = jnp.swapaxes(w_gate, 1, 2), jnp.swapaxes(w_up, 1, 2)
        kc = k_cache.reshape(layers, rows * seq, head)
        vc = v_cache.reshape(layers, rows * seq, head)
        return block_call(layers, rows, width, cw, groups, head, seq, ff)(
            x_in, lens, table, norm_gain, w_q, w_k, w_v, gate_t, up_t, w_o, w_down, kc, vc)

    return jax.shard_map(per_device, mesh=mesh, in_specs=arg_specs, out_specs=P("dp", None), check_vma=False)
```

time: 202 us -> 189 us (0.936)
  Pallas kernels: 196 us -> 182 us
    pallas_call x1, Pallas kernels: 196 us -> 182 us  [per_device(): block_call(layers, rows, width, cw, groups, head, seq, ff)]
where the time goes in v5:
time: 189 us; the launch traced here: 188 us
  Pallas kernels  182 us (96%)
  local copies, waits for them, and re-layouts  6.02 us (3%)
    pallas_call x1, Pallas kernels, per_device(): block_call(layers, rows, width, cw, groups, head, seq, ff)  182 us
    unnamed x1, local copies, waits for them, and re-layouts  5.18 us

profile of v5, /device:TPU:0, one launch (start us, length us, event | category | flops | bytes accessed | tf_op | source)
XLA Modules:
  0.0 188.5 jit_solution(66983477054142248)
XLA Ops:
  0.0 0.7 convert_element_type.3
  0.7 0.8 broadcast_in_dim.2.lens
  1.5 181.7 %mega.1 = bf16[512,5120]{1,0:T(8,128)(2,1)} custom-call(bf16[512,5120]{1,0:T(8,128)(2,1)} %x_hbm.1, f32[512,128]{1,0:T(8,128)} %broadcast_in_dim.2.lens, f32[128,256]{1,0:T(8,128)} %constant.2.clone.table, bf16[2,5120]{1,0:T(2,128)(2,1)} %gain.1, bf16[2,5120,640]{2,1,0:T(8,128)(2,1)} %wq.1, bf16[2,5120,128]{2,1,0:T(8,128)(2,1)} %wk.1, ...), custom_call_target="tpu_custom_call" | custom-call | tf_op jit(solution)/shard_map/mega/pallas_call | solution.py:539
  183.3 5.2 %copy.15 = bf16[512,5120]{1,0:T(8,128)(2,1)} copy(bf16[512,5120]{1,0:T(8,128)(2,1)} %mega.1) | data formatting | bytes 10485760
